TPU v7x, 128 devices: a whole 4x4x4 slice. The times are simulated.
128 devices in a mesh: tm: 16 (over y_hi, z, core), bank: 8 (over y_lo, x).
Axes of the slice: x: 4, y: 4 (y_hi: 2, y_lo: 2; y = y_hi * 2 + y_lo), z: 4, core: 2. Of those that a mesh axis runs over, the one named last changes fastest.
Arguments:
- strain: float32 [32, 131072], P('tm', 'bank'), may hold values from -40 to 40
- lengths: int32 [32], P('tm'), may hold values from 65536 to 131072
- templates: bfloat16 [2, 32, 512, 512], P(None, 'bank'), may hold values from -6 to 6
Outputs:
- snr: float32 [32, 4194304], P('bank', 'tm')
All inputs are finite; a program needn't handle non-finite values.
Results may differ from a plain program's by a relative error of at most 0.014.
Values may be sent and summed in bfloat16 or wider, within the bound.
A program may use at most 128 MiB of HBM per device.

v0:
```python
import functools
import math

import jax
import jax.numpy as jnp
import numpy as np
from jax import lax
from jax.experimental import pallas as pl
from jax.experimental.pallas import tpu as pltpu
from jax.sharding import PartitionSpec as P

R = 512
HALF = 256
ROWS = 272
RADIX = 4
Q = 128
epsilon = 1e-06
MESH = pl.DeviceIdType.MESH


def tables():
    k = np.arange(HALF + 1, dtype=np.int64)
    u = np.arange(R, dtype=np.int64)
    angle = 2.0 * math.pi * ((k[:, None] * u[None, :]) % R) / R
    first = np.zeros((2 * ROWS, R), np.float64)
    first[: HALF + 1] = np.cos(angle)
    first[ROWS : ROWS + HALF + 1] = -np.sin(angle)
    turn = 2.0 * math.pi * (k[:, None] * u[None, :]) / (R * R)
    tc = np.zeros((ROWS, R), np.float64)
    ts = np.zeros((ROWS, R), np.float64)
    tc[: HALF + 1] = np.cos(turn)
    ts[: HALF + 1] = np.sin(turn)
    v = np.arange(Q, dtype=np.int64)
    fwd = np.zeros((RADIX, HALF, HALF), np.float64)
    inv = np.zeros((RADIX, HALF, HALF), np.float64)
    for r in range(RADIX):
        phase = 2.0 * math.pi * ((v[:, None] * (RADIX * v[None, :] + r)) % R) / R
        c, s = np.cos(phase), np.sin(phase)
        fwd[r] = np.block([[c, -s], [s, c]])
        inv[r] = np.block([[c.T, s.T], [-s.T, c.T]])
    w = np.arange(HALF, dtype=np.int64)
    last = np.zeros((HALF, R), np.float64)
    phase = 2.0 * math.pi * ((w[:, None] * k[None, :HALF]) % R) / R
    last[:, :HALF] = np.cos(phase)
    last[:, HALF:] = -np.sin(phase)
    last[:, HALF] = 1.0 - 2.0 * (w % 2)
    return first, tc, ts, fwd, inv, last


def half(x):
    return x.astype(jnp.bfloat16)


def full(x):
    return x.astype(jnp.float32)


def dot(a, b):
    return jnp.dot(a, b, preferred_element_type=jnp.float32)


CHUNKS = ((0, 128), (128, 144))


def inverse_kernel(z_ref, g_ref, fac_ref, inv_ref, tc_ref, ts_ref, last_ref, out_ref, back, y, sem):
    j = pl.program_id(0)
    slot = lax.rem(j, 2)

    def copies(at, which):
        return [
            pltpu.make_async_copy(
                y.at[which, q, :, pl.ds(m * Q, Q)],
                out_ref.at[pl.ds(q * HALF, HALF), m, at, :],
                sem.at[which, q * RADIX + m],
            )
            for q in range(2)
            for m in range(RADIX)
        ]

    @pl.when(j >= 2)
    def _():
        for c in copies(j - 2, slot):
            c.wait()

    factor = fac_ref[0, 0:1, 0:1]
    for q in range(2):
        for start, size in CHUNKS:
            rows = pl.ds(start, size)
            tr, ti = [], []
            for r in range(RADIX):
                lo = r * 2 * Q
                zr = full(z_ref[q, rows, lo : lo + Q])
                zi = full(z_ref[q, rows, lo + Q : lo + 2 * Q])
                gr = full(g_ref[0, rows, lo : lo + Q])
                gi = full(g_ref[0, rows, lo + Q : lo + 2 * Q])
                prod = jnp.concatenate([half(gr * zr + gi * zi), half(gr * zi - gi * zr)], axis=1)
                t = dot(prod, inv_ref[r])
                tr.append(t[:, :Q])
                ti.append(t[:, Q:])
            ar, ai, br, bi = tr[0] + tr[2], ti[0] + ti[2], tr[0] - tr[2], ti[0] - ti[2]
            cr, ci, dr, di = tr[1] + tr[3], ti[1] + ti[3], tr[1] - tr[3], ti[1] - ti[3]
            inner = ((ar + cr, ai + ci), (br - di, bi + dr), (ar - cr, ai - ci), (br + di, bi - dr))
            for m in range(RADIX):
                lanes = slice(m * Q, (m + 1) * Q)
                ir, ii = inner[m]
                tc, ts = tc_ref[rows, lanes], ts_ref[rows, lanes]
                real = half(ir * tc - ii * ts)
                imag = half(ii * tc + ir * ts)
                keep = min(size, HALF - start)
                back[q, pl.ds(start, keep), lanes] = real[:keep]
                if start == 0:
                    back[q, pl.ds(HALF, keep), lanes] = imag[:keep]
                else:
                    back[q, pl.ds(HALF + start, keep), lanes] = imag[:keep]
                    top = back[q, HALF : HALF + 16, lanes]
                    first_row = lax.broadcasted_iota(jnp.int32, (16, Q), 0) == 0
                    back[q, HALF : HALF + 16, lanes] = half(
                        jnp.where(first_row, full(real[keep : keep + 16]), full(top))
                    )
        y[slot, q] = dot(last_ref[...], back[q]) * factor

    for c in copies(j, slot):
        c.start()

    @pl.when(j == pl.num_programs(0) - 1)
    def _():
        for c in copies(j - 1, 1 - slot):
            c.wait()
        for c in copies(j, slot):
            c.wait()


def inverse(z, g, fac, inv, tc, ts, last):
    n = g.shape[0]
    whole = lambda *shape: pl.BlockSpec(shape, lambda j: (0,) * len(shape))
    return pl.pallas_call(
        inverse_kernel,
        grid=(n,),
        in_specs=[
            whole(2, ROWS, 2 * R),
            pl.BlockSpec((1, ROWS, 2 * R), lambda j: (j, 0, 0)),
            pl.BlockSpec((1, 8, Q), lambda j: (j, 0, 0)),
            whole(RADIX, HALF, HALF),
            whole(ROWS, R),
            whole(ROWS, R),
            whole(HALF, R),
        ],
        out_specs=pl.BlockSpec(memory_space=pl.ANY),
        out_shape=jax.ShapeDtypeStruct((2 * HALF, RADIX, n, Q), jnp.float32),
        scratch_shapes=[
            pltpu.VMEM((2, R, R), jnp.bfloat16),
            pltpu.VMEM((2, 2, HALF, R), jnp.float32),
            pltpu.SemaphoreType.DMA((2, 2 * RADIX)),
        ],
        compiler_params=pltpu.CompilerParams(vmem_limit_bytes=32 << 20),
        name="inverse",
    )(z, g, fac, inv, tc, ts, last)


def fill_slot(i, lanes):
    return slice(i * lanes, (i + 1) * lanes)


def forward(fr, fi, tc, ts, fwd_ref):
    tr = fr * tc + fi * ts
    ti = fi * tc - fr * ts
    r0, r1, r2, r3 = (tr[:, fill_slot(m, Q)] for m in range(RADIX))
    i0, i1, i2, i3 = (ti[:, fill_slot(m, Q)] for m in range(RADIX))
    ar, ai, br, bi = r0 + r2, i0 + i2, r0 - r2, i0 - i2
    cr, ci, dr, di = r1 + r3, i1 + i3, r1 - r3, i1 - i3
    parts = ((ar + cr, ai + ci), (br + di, bi - dr), (ar - cr, ai - ci), (br - di, bi + dr))
    return [
        dot(jnp.concatenate([half(x), half(y)], axis=1), fwd_ref[r])
        for r, (x, y) in enumerate(parts)
    ]


def spectrum_kernel(
    tm, bank, total_blocks,
    strain_ref, lens_ref, tmpl_hbm, first_hbm, tc_hbm, ts_hbm, fwd_hbm,
    z_ref, g_ref, fac_ref,
    raw, blocks, prev, tmpl, first, tc, ts, fwd, zraw, send, recv, weights,
    load_sem, gather_send, gather_recv, sum_send, sum_recv, prev_send, prev_recv,
    share_send, share_recv,
):
    t = lax.axis_index("tm")
    b = lax.axis_index("bank")
    piece = HALF // bank
    band = HALF // bank
    tiles = band // 8 * RADIX

    loads = []
    for c in range(2):
        for m in range(RADIX):
            loads.append((strain_ref.at[:, m, c, :], raw.at[c, :, pl.ds(m * Q, Q)]))
    loads += [(first_hbm, first), (tc_hbm, tc), (ts_hbm, ts), (fwd_hbm, fwd), (tmpl_hbm, tmpl)]
    loads = [pltpu.make_async_copy(s, d, load_sem.at[i]) for i, (s, d) in enumerate(loads)]
    for load in loads:
        load.start()

    barrier = pltpu.get_barrier_semaphore()
    for i in range(1, bank):
        pl.semaphore_signal(
            barrier, 1, device_id={"tm": t, "bank": lax.rem(b + i, bank)}, device_id_type=MESH
        )
    for i in range(1, tm):
        pl.semaphore_signal(
            barrier, 1, device_id={"tm": lax.rem(t + i, tm), "bank": b}, device_id_type=MESH
        )

    for load in loads[: 2 * RADIX]:
        load.wait()
    own_rows = pl.ds(pl.multiple_of(b * piece, piece), piece)
    position = (
        (lax.broadcasted_iota(jnp.int32, (piece, R), 0) + b * piece) * R
        + lax.broadcasted_iota(jnp.int32, (piece, R), 1)
    )
    for c in range(2):
        blocks[c, own_rows, :] = half(jnp.where(position < lens_ref[c], raw[c], 0.0))

    @pl.when(t == 0)
    def _():
        prev[...] = jnp.zeros_like(prev)

    pl.semaphore_wait(barrier, bank + tm - 2)

    def gather_copy(i):
        return pltpu.make_async_remote_copy(
            src_ref=blocks.at[:, own_rows, :],
            dst_ref=blocks.at[:, own_rows, :],
            send_sem=gather_send.at[i],
            recv_sem=gather_recv.at[i],
            device_id={"tm": t, "bank": lax.rem(b + i, bank)},
            device_id_type=MESH,
        )

    def gather_arrival(i):
        source = lax.rem(b - i + bank, bank)
        rows = pl.ds(pl.multiple_of(source * piece, piece), piece)
        return pltpu.make_async_remote_copy(
            src_ref=blocks.at[:, rows, :],
            dst_ref=blocks.at[:, rows, :],
            send_sem=gather_send.at[i],
            recv_sem=gather_recv.at[i],
            device_id={"tm": t, "bank": source},
            device_id_type=MESH,
        )

    for i in range(1, bank):
        gather_copy(i).start()

    for load in loads[2 * RADIX :]:
        load.wait()
    row = lax.broadcasted_iota(jnp.int32, (R, R), 0)
    col = lax.broadcasted_iota(jnp.int32, (R, R), 1)
    order = lax.rem(col, Q) * RADIX + lax.div(col, Q)
    pick = half(jnp.where(row == order, 1.0, 0.0))
    pick_mirror = half(jnp.where(row == R - 1 - order, 1.0, 0.0))
    up = lax.broadcasted_iota(jnp.int32, (ROWS, HALF), 0)
    across = lax.broadcasted_iota(jnp.int32, (ROWS, HALF), 1)
    flip = half(jnp.where(jnp.logical_and(across == HALF - up, across > 0), 1.0, 0.0))

    def join(j, carry):
        norm = jnp.zeros((1, R), jnp.float32)
        for p in range(2):
            direct = dot(tmpl[p, j, 0:ROWS, :], pick)
            mirror = dot(flip, half(dot(tmpl[p, j, HALF:R, :], pick_mirror)))
            joined = half(direct + mirror if p == 0 else direct - mirror)
            for r in range(RADIX):
                lo = (2 * r + p) * Q
                g_ref[j, :, lo : lo + Q] = joined[:, fill_slot(r, Q)]
            values = full(tmpl[p, j])
            norm = norm + jnp.sum(values * values, axis=0, keepdims=True)
        factor = lax.rsqrt(jnp.sum(norm, axis=1, keepdims=True))
        fac_ref[j] = jnp.broadcast_to(factor, (8, Q))
        return carry

    lax.fori_loop(0, g_ref.shape[0], join, 0)

    for i in range(1, bank):
        gather_arrival(i).wait_recv()

    low = pl.ds(pl.multiple_of(b * band, band), band)
    low_imag = pl.ds(pl.multiple_of(ROWS + b * band, 16), band)
    table = jnp.concatenate(
        [
            first[low, 0:HALF],
            first[HALF:ROWS, 0:HALF],
            first[low_imag, 0:HALF],
            first[ROWS + HALF : 2 * ROWS, 0:HALF],
        ],
        axis=0,
    )
    band_tc = jnp.concatenate([tc[low, :], tc[HALF:ROWS, :]], axis=0)
    band_ts = jnp.concatenate([ts[low, :], ts[HALF:ROWS, :]], axis=0)
    power = [0.0] * RADIX
    height = band + ROWS - HALF
    for c in range(2):
        f = dot(table, blocks[c])
        spec = forward(f[:height], f[height:], band_tc, band_ts, fwd)
        for r in range(RADIX):
            re, im = spec[r][:, :Q], spec[r][:, Q:]
            power[r] = power[r] + (re * re + im * im)
    extra = jnp.concatenate(
        [power[r][band : band + 1] for r in range(RADIX)] + [jnp.zeros((8 - RADIX, Q), jnp.float32)],
        axis=0,
    )
    for i in range(tiles):
        at = i // RADIX * 8
        send[i, 0:8, :] = power[i % RADIX][at : at + 8]
        send[i, 8:16, :] = extra

    def sum_copy(i):
        to = lax.rem(t + i, tm)
        return pltpu.make_async_remote_copy(
            src_ref=send.at[to],
            dst_ref=recv.at[t],
            send_sem=sum_send.at[i],
            recv_sem=sum_recv.at[i],
            device_id={"tm": to, "bank": b},
            device_id_type=MESH,
        )

    def sum_arrival(i):
        source = lax.rem(t - i + tm, tm)
        return pltpu.make_async_remote_copy(
            src_ref=send.at[source],
            dst_ref=recv.at[source],
            send_sem=sum_send.at[i],
            recv_sem=sum_recv.at[i],
            device_id={"tm": source, "bank": b},
            device_id_type=MESH,
        )

    for i in range(1, tm):
        sum_copy(i).start()
    recv[t] = send[t]

    next_copy = pltpu.make_async_remote_copy(
        src_ref=blocks.at[1],
        dst_ref=prev,
        send_sem=prev_send,
        recv_sem=prev_recv,
        device_id={"tm": lax.rem(t + 1, tm), "bank": b},
        device_id_type=MESH,
    )

    @pl.when(t < tm - 1)
    def _():
        next_copy.start()

    def region(q, now, before):
        f = dot(first[:, 0:HALF], now) + dot(first[:, HALF:R], before)
        spec = forward(f[:ROWS], f[ROWS:], tc[...], ts[...], fwd)
        for r in range(RADIX):
            zraw[q, :, fill_slot(r, 2 * Q)] = spec[r]

    region(1, blocks[1], blocks[0])

    for i in range(1, tm):
        sum_arrival(i).wait_recv()
    total = recv[0]
    for i in range(1, tm):
        total = total + recv[i]
    weight = lax.rsqrt(total * (1.0 / total_blocks) + epsilon)
    me = b * tm + t
    weights[me] = half(weight[0:8])

    def share_copy(to_t, to_b, slot):
        return pltpu.make_async_remote_copy(
            src_ref=weights.at[slot],
            dst_ref=weights.at[slot],
            send_sem=share_send,
            recv_sem=share_recv,
            device_id={"tm": to_t, "bank": to_b},
            device_id_type=MESH,
        )

    def share(i, carry):
        share_copy(lax.rem(t + lax.div(i, bank), tm), lax.rem(b + lax.rem(i, bank), bank), me).start()
        return carry

    lax.fori_loop(1, tm * bank, share, 0)

    @pl.when(t > 0)
    def _():
        next_copy.wait_recv()

    region(0, blocks[0], prev[...])

    others = pltpu.make_async_remote_copy(
        src_ref=weights.at[pl.ds(0, tm * bank - 1)],
        dst_ref=weights.at[pl.ds(0, tm * bank - 1)],
        send_sem=share_send,
        recv_sem=share_recv,
        device_id={"tm": t, "bank": lax.rem(b + 1, bank)},
        device_id_type=MESH,
    )
    others.wait_recv()

    def whiten(i, carry):
        rows = pl.ds(pl.multiple_of(i * 16, 16), 16)
        for r in range(RADIX):
            at = 2 * i * RADIX + r
            w = jnp.concatenate([full(weights[at]), full(weights[at + RADIX])], axis=0)
            for q in range(2):
                for p in range(2):
                    lanes = fill_slot(2 * r + p, Q)
                    z_ref[q, rows, lanes] = half(zraw[q, rows, lanes] * w)
        return carry

    lax.fori_loop(0, HALF // 16, whiten, 0)
    for r in range(RADIX):
        for q in range(2):
            for p in range(2):
                lanes = fill_slot(2 * r + p, Q)
                z_ref[q, HALF:ROWS, lanes] = half(
                    zraw[q, HALF:ROWS, lanes] * weight[8 + r : 9 + r]
                )

    for i in range(1, bank):
        gather_copy(i).wait_send()
    for i in range(1, tm):
        sum_copy(i).wait_send()

    @pl.when(t < tm - 1)
    def _():
        next_copy.wait_send()

    others.wait_send()


def spectra(strain, lengths, templates, tabs, tm, bank):
    n = templates.shape[1]
    first, tc, ts, fwd = tabs
    anyspace = pl.BlockSpec(memory_space=pl.ANY)
    vmem = pl.BlockSpec(memory_space=pltpu.VMEM)
    bf, f32 = jnp.bfloat16, jnp.float32
    sem = pltpu.SemaphoreType.DMA
    pieces = strain.reshape(2, HALF // bank * RADIX, Q).transpose(1, 0, 2)
    pieces = pieces.reshape(HALF // bank, RADIX, 2, Q)
    return pl.pallas_call(
        functools.partial(spectrum_kernel, tm, bank, 2 * tm),
        in_specs=[anyspace, pl.BlockSpec(memory_space=pltpu.SMEM)] + [anyspace] * 5,
        out_specs=[vmem] * 3,
        out_shape=[
            jax.ShapeDtypeStruct((2, ROWS, 2 * R), bf),
            jax.ShapeDtypeStruct((n, ROWS, 2 * R), bf),
            jax.ShapeDtypeStruct((n, 8, Q), f32),
        ],
        scratch_shapes=[
            pltpu.VMEM((2, HALF // bank, R), f32),
            pltpu.VMEM((2, HALF, R), bf),
            pltpu.VMEM((HALF, R), bf),
            pltpu.VMEM((2, n, R, R), bf),
            pltpu.VMEM((2 * ROWS, R), bf),
            pltpu.VMEM((ROWS, R), f32),
            pltpu.VMEM((ROWS, R), f32),
            pltpu.VMEM((RADIX, HALF, HALF), bf),
            pltpu.VMEM((2, ROWS, 2 * R), f32),
            pltpu.VMEM((tm, 16, Q), f32),
            pltpu.VMEM((tm, 16, Q), f32),
            pltpu.VMEM((tm * bank, 8, Q), bf),
            sem((2 * RADIX + 5,)),
            sem((bank,)),
            sem((bank,)),
            sem((tm,)),
            sem((tm,)),
            sem,
            sem,
            sem,
            sem,
        ],
        compiler_params=pltpu.CompilerParams(
            collective_id=0, has_side_effects=True, vmem_limit_bytes=32 << 20
        ),
        name="spectra",
    )(pieces, lengths, templates, first, tc, ts, fwd)


def body(tm, bank, strain, lengths, templates):
    first, tc, ts, fwd, inv, last = tables()
    bf = lambda x: jnp.asarray(x, jnp.bfloat16)
    f32 = lambda x: jnp.asarray(x, jnp.float32)
    tc, ts = f32(tc), f32(ts)
    z, g, fac = spectra(strain, lengths, templates, (bf(first), tc, ts, bf(fwd)), tm, bank)
    out = inverse(z, g, fac, bf(inv), tc, ts, bf(last))
    n = templates.shape[1]
    return out.reshape(2 * HALF * RADIX, n, Q).transpose(1, 0, 2).reshape(n, 2 * HALF * R)


def solution(mesh):
    in_specs = (P("tm", "bank"), P("tm"), P(None, "bank", None, None))
    step = functools.partial(body, mesh.shape["tm"], mesh.shape["bank"])
    return jax.shard_map(
        step, mesh=mesh, in_specs=in_specs, out_specs=P("bank", "tm"), check_vma=False
    )
```

profile of v0, /device:TPU:1, one launch (start us, length us, event | category | flops | bytes accessed | tf_op | source)
XLA Modules:
  0.0 47.2 jit_solution(15947111521071946505)
XLA Ops:
  0.0 0.0 copy-start
  0.0 2.2 %copy-done = bf16[2,4,512,512]{3,2,1,0:T(8,128)(2,1)S(1)} copy-done((bf16[2,4,512,512]{3,2,1,0:T(8,128)(2,1)S(1)}, bf16[2,4,512,512]{3,2,1,0:T(8,128)(2,1)}, u32[]{:S(2)}) %copy-start) | copy-done | bytes 4194328
  2.2 0.0 copy-start.1
  2.2 1.1 %copy-done.1 = f32[272,512]{1,0:T(8,128)S(1)} copy-done((f32[272,512]{1,0:T(8,128)S(1)}, f32[272,512]{1,0:T(8,128)}, u32[]{:S(2)}) %copy-start.1) | copy-done | bytes 557080
  3.2 0.0 copy-start.2
  3.2 1.1 %copy-done.2 = f32[272,512]{1,0:T(8,128)S(1)} copy-done((f32[272,512]{1,0:T(8,128)S(1)}, f32[272,512]{1,0:T(8,128)}, u32[]{:S(2)}) %copy-start.2) | copy-done | bytes 557080
  4.3 0.0 copy-start.4
  4.3 1.1 %copy-done.4 = bf16[544,512]{1,0:T(8,128)(2,1)S(1)} copy-done((bf16[544,512]{1,0:T(8,128)(2,1)S(1)}, bf16[544,512]{1,0:T(8,128)(2,1)}, u32[]{:S(2)}) %copy-start.4) | copy-done | bytes 557080
  5.3 0.0 copy-start.6
  5.4 1.0 %copy-done.6 = bf16[4,256,256]{2,1,0:T(8,128)(2,1)S(1)} copy-done((bf16[4,256,256]{2,1,0:T(8,128)(2,1)S(1)}, bf16[4,256,256]{2,1,0:T(8,128)(2,1)}, u32[]{:S(2)}) %copy-start.6) | copy-done | bytes 524312
  6.4 0.0 copy-start.8
  6.4 0.9 %copy-done.8 = f32[2,16384]{1,0:T(2,128)S(1)} copy-done((f32[2,16384]{1,0:T(2,128)S(1)}, f32[2,16384]{1,0:T(2,128)}, u32[]{:S(2)}) %copy-start.8) | copy-done | bytes 131096
  7.3 0.0 copy-start.9
  7.3 0.7 %copy-done.9 = s32[2]{0:T(128)S(1)} copy-done((s32[2]{0:T(128)S(1)}, s32[2]{0:T(128)}, u32[]{:S(2)}) %copy-start.9) | copy-done | bytes 32
  8.0 0.0 copy-start.3
  8.0 0.0 copy-start.5
  8.0 0.0 copy-start.7
  8.0 32.2 %spectra.1 = (bf16[2,272,1024]{2,1,0:T(8,128)(2,1)S(1)}, bf16[4,272,1024]{2,1,0:T(8,128)(2,1)S(1)}, f32[4,8,128]{2,1,0:T(8,128)S(1)}) custom-call(f32[32,4,2,128]{3,2,1,0:T(2,128)S(1)} %bitcast.10, s32[2]{0:T(128)S(1)} %copy-done.9, bf16[2,4,512,512]{3,2,1,0:T(8,128)(2,1)S(1)} %copy-done, bf16[544,512]{1,0:T(8,128)(2,1)S(1)} %copy-done.4, ...), custom_call_target="tpu_custom_call" | custom-call | tf_op jit(solution)/shard_map/spectra/pallas_call | solution.py:442
  40.2 0.0 copy-done.3
  40.2 0.0 copy-done.5
  40.2 0.0 copy-done.7
  40.2 7.0 %inverse.1 = f32[512,4,4,128]{3,2,1,0:T(4,128)} custom-call(bf16[2,272,1024]{2,1,0:T(8,128)(2,1)S(1)} %get-tuple-element.8.z_ref, bf16[4,272,1024]{2,1,0:T(8,128)(2,1)S(1)} %get-tuple-element.9.g_ref, f32[4,8,128]{2,1,0:T(8,128)S(1)} %get-tuple-element.10.fac_ref, bf16[4,256,256]{2,1,0:T(8,128)(2,1)S(1)} %copy-done.5, f32[272,512]{1,0:T(8,128)S(1)} %copy-done.3, ...), custom_call_target="tpu_custom_call" | custom-call | tf_op jit(solution)/shard_map/inverse/pallas_call | solution.py:136
Async XLA Ops:
  0.0 2.2 %copy-start = (bf16[2,4,512,512]{3,2,1,0:T(8,128)(2,1)S(1)}, bf16[2,4,512,512]{3,2,1,0:T(8,128)(2,1)}, u32[]{:S(2)}) copy-start(bf16[2,4,512,512]{3,2,1,0:T(8,128)(2,1)} %tmpl_hbm.1) | copy-start | bytes 12582916
  2.2 1.1 %copy-start.1 = (f32[272,512]{1,0:T(8,128)S(1)}, f32[272,512]{1,0:T(8,128)}, u32[]{:S(2)}) copy-start(f32[272,512]{1,0:T(8,128)} %constant.13.clone.ts_hbm.ts_ref) | copy-start | bytes 1671172
  3.2 1.1 %copy-start.2 = (f32[272,512]{1,0:T(8,128)S(1)}, f32[272,512]{1,0:T(8,128)}, u32[]{:S(2)}) copy-start(f32[272,512]{1,0:T(8,128)} %constant.12.clone.tc_hbm.tc_ref) | copy-start | bytes 1671172
  4.3 1.1 %copy-start.4 = (bf16[544,512]{1,0:T(8,128)(2,1)S(1)}, bf16[544,512]{1,0:T(8,128)(2,1)}, u32[]{:S(2)}) copy-start(bf16[544,512]{1,0:T(8,128)(2,1)} %constant.14.clone.first_hbm) | copy-start | bytes 1671172
  5.3 1.0 %copy-start.6 = (bf16[4,256,256]{2,1,0:T(8,128)(2,1)S(1)}, bf16[4,256,256]{2,1,0:T(8,128)(2,1)}, u32[]{:S(2)}) copy-start(bf16[4,256,256]{2,1,0:T(8,128)(2,1)} %constant.15.clone.fwd_hbm) | copy-start | bytes 1572868
  6.4 0.9 %copy-start.8 = (f32[2,16384]{1,0:T(2,128)S(1)}, f32[2,16384]{1,0:T(2,128)}, u32[]{:S(2)}) copy-start(f32[2,16384]{1,0:T(2,128)} %param.9) | copy-start | bytes 393220
  7.3 0.7 %copy-start.9 = (s32[2]{0:T(128)S(1)}, s32[2]{0:T(128)}, u32[]{:S(2)}) copy-start(s32[2]{0:T(128)} %lens_ref.1) | copy-start | bytes 28
  8.0 32.2 %copy-start.3 = (f32[272,512]{1,0:T(8,128)S(1)}, f32[272,512]{1,0:T(8,128)}, u32[]{:S(2)}) copy-start(f32[272,512]{1,0:T(8,128)} %constant.12.clone.tc_hbm.tc_ref) | copy-start | bytes 1671172
  8.0 32.3 %copy-start.5 = (bf16[4,256,256]{2,1,0:T(8,128)(2,1)S(1)}, bf16[4,256,256]{2,1,0:T(8,128)(2,1)}, u32[]{:S(2)}) copy-start(bf16[4,256,256]{2,1,0:T(8,128)(2,1)} %constant.16.clone.inv_ref) | copy-start | bytes 1572868
  8.0 32.3 %copy-start.7 = (bf16[256,512]{1,0:T(8,128)(2,1)S(1)}, bf16[256,512]{1,0:T(8,128)(2,1)}, u32[]{:S(2)}) copy-start(bf16[256,512]{1,0:T(8,128)(2,1)} %constant.17.clone.last_ref) | copy-start | bytes 786436
where the time goes:
time: 47.6 us; the launch traced here: 47.2 us
  Pallas kernels  39.2 us (82%)
  local copies, waits for them, and re-layouts  7.96 us (17%)
    pallas_call x1, Pallas kernels, spectra(): pl.pallas_call(functools.partial(spectrum_kernel, tm, bank, 2 * tm), in_s...  32.2 us
    unnamed x20, local copies, waits for them, and re-layouts  7.96 us
    pallas_call x1, Pallas kernels, inverse(): pl.pallas_call(inverse_kernel, grid=(n,), in_specs=[whole(2, ROWS, 2 * R)...  6.97 us

commit v1 on v0

--- a/solution.py
+++ b/solution.py
@@ -177,9 +177,9 @@
 
 def spectrum_kernel(
     tm, bank, total_blocks,
-    strain_ref, lens_ref, tmpl_hbm, first_hbm, tc_hbm, ts_hbm, fwd_hbm,
+    strain_ref, lens_hbm, tmpl_hbm, first_hbm, tc_hbm, ts_hbm, fwd_hbm,
     z_ref, g_ref, fac_ref,
-    raw, blocks, prev, tmpl, first, tc, ts, fwd, zraw, send, recv, weights,
+    lens_ref, raw, blocks, prev, tmpl, first, tc, ts, fwd, zraw, send, recv, weights,
     load_sem, gather_send, gather_recv, sum_send, sum_recv, prev_send, prev_recv,
     share_send, share_recv,
 ):
@@ -189,7 +189,7 @@
     band = HALF // bank
     tiles = band // 8 * RADIX
 
-    loads = []
+    loads = [(lens_hbm, lens_ref)]
     for c in range(2):
         for m in range(RADIX):
             loads.append((strain_ref.at[:, m, c, :], raw.at[c, :, pl.ds(m * Q, Q)]))
@@ -208,7 +208,7 @@
             barrier, 1, device_id={"tm": lax.rem(t + i, tm), "bank": b}, device_id_type=MESH
         )
 
-    for load in loads[: 2 * RADIX]:
+    for load in loads[: 2 * RADIX + 1]:
         load.wait()
     own_rows = pl.ds(pl.multiple_of(b * piece, piece), piece)
     position = (
@@ -249,7 +249,7 @@
     for i in range(1, bank):
         gather_copy(i).start()
 
-    for load in loads[2 * RADIX :]:
+    for load in loads[2 * RADIX + 1 :]:
         load.wait()
     row = lax.broadcasted_iota(jnp.int32, (R, R), 0)
     col = lax.broadcasted_iota(jnp.int32, (R, R), 1)
@@ -433,7 +433,7 @@
 def spectra(strain, lengths, templates, tabs, tm, bank):
     n = templates.shape[1]
     first, tc, ts, fwd = tabs
-    anyspace = pl.BlockSpec(memory_space=pl.ANY)
+    hbm = pl.BlockSpec(memory_space=pltpu.HBM)
     vmem = pl.BlockSpec(memory_space=pltpu.VMEM)
     bf, f32 = jnp.bfloat16, jnp.float32
     sem = pltpu.SemaphoreType.DMA
@@ -441,7 +441,7 @@
     pieces = pieces.reshape(HALF // bank, RADIX, 2, Q)
     return pl.pallas_call(
         functools.partial(spectrum_kernel, tm, bank, 2 * tm),
-        in_specs=[anyspace, pl.BlockSpec(memory_space=pltpu.SMEM)] + [anyspace] * 5,
+        in_specs=[hbm] * 7,
         out_specs=[vmem] * 3,
         out_shape=[
             jax.ShapeDtypeStruct((2, ROWS, 2 * R), bf),
@@ -449,6 +449,7 @@
             jax.ShapeDtypeStruct((n, 8, Q), f32),
         ],
         scratch_shapes=[
+            pltpu.SMEM((2,), jnp.int32),
             pltpu.VMEM((2, HALF // bank, R), f32),
             pltpu.VMEM((2, HALF, R), bf),
             pltpu.VMEM((HALF, R), bf),
@@ -461,7 +462,7 @@
             pltpu.VMEM((tm, 16, Q), f32),
             pltpu.VMEM((tm, 16, Q), f32),
             pltpu.VMEM((tm * bank, 8, Q), bf),
-            sem((2 * RADIX + 5,)),
+            sem((2 * RADIX + 6,)),
             sem((bank,)),
             sem((bank,)),
             sem((tm,)),
@@ -475,7 +476,7 @@
             collective_id=0, has_side_effects=True, vmem_limit_bytes=32 << 20
         ),
         name="spectra",
-    )(pieces, lengths, templates, first, tc, ts, fwd)
+    )(*[pltpu.with_memory_space_constraint(x, pltpu.HBM) for x in (pieces, lengths, templates, first, tc, ts, fwd)])
 
 
 def body(tm, bank, strain, lengths, templates):

time: 47.6 us -> 38 us (0.80)
  local copies, waits for them, and re-layouts: 7.96 us -> 0.02 us
  Pallas kernels: 39.2 us -> 37.9 us
    unnamed x20 -> x8, local copies, waits for them, and re-layouts: 7.96 us -> 0.02 us
    pallas_call x1, Pallas kernels: 32.2 us -> 31.2 us  [spectra(): pl.pallas_call(functools.partial(spectrum_kernel, tm, bank, 2 * tm), in_s...]
where the time goes in v1:
time: 38 us; the launch traced here: 37.9 us
  Pallas kernels  37.9 us (100%)
    pallas_call x1, Pallas kernels, spectra(): pl.pallas_call(functools.partial(spectrum_kernel, tm, bank, 2 * tm), in_s...  31.2 us
    pallas_call x1, Pallas kernels, inverse(): pl.pallas_call(inverse_kernel, grid=(n,), in_specs=[whole(2, ROWS, 2 * R)...  6.68 us

profile of v1, /device:TPU:1, one launch (start us, length us, event | category | flops | bytes accessed | tf_op | source)
XLA Modules:
  0.0 37.9 jit_solution(14179657161577364168)
XLA Ops:
  0.0 0.0 copy-start
  0.0 0.0 copy-start.1
  0.0 0.0 copy-start.3
  0.0 0.0 copy-start.2
  0.0 31.2 %spectra.1 = (bf16[2,272,1024]{2,1,0:T(8,128)(2,1)S(1)}, bf16[4,272,1024]{2,1,0:T(8,128)(2,1)S(1)}, f32[4,8,128]{2,1,0:T(8,128)S(1)}) custom-call(f32[32,4,2,128]{3,2,1,0:T(2,128)} %bitcast.10, s32[2]{0:T(128)} %lens_hbm.1, bf16[2,4,512,512]{3,2,1,0:T(8,128)(2,1)} %tmpl_hbm.1, bf16[544,512]{1,0:T(8,128)(2,1)} %constant.14.clone.first_hbm, ...), custom_call_target="tpu_custom_call" | custom-call | tf_op jit(solution)/shard_map/spectra/pallas_call | solution.py:442
  31.2 0.0 copy-done
  31.2 0.0 copy-done.1
  31.2 0.0 copy-done.3
  31.2 0.0 copy-done.2
  31.2 6.7 %inverse.1 = f32[512,4,4,128]{3,2,1,0:T(4,128)} custom-call(bf16[2,272,1024]{2,1,0:T(8,128)(2,1)S(1)} %get-tuple-element.8.z_ref, bf16[4,272,1024]{2,1,0:T(8,128)(2,1)S(1)} %get-tuple-element.9.g_ref, f32[4,8,128]{2,1,0:T(8,128)S(1)} %get-tuple-element.10.fac_ref, bf16[4,256,256]{2,1,0:T(8,128)(2,1)S(1)} %copy-done.2, f32[272,512]{1,0:T(8,128)S(1)} %copy-done.1, ...), custom_call_target="tpu_custom_call" | custom-call | tf_op jit(solution)/shard_map/inverse/pallas_call | solution.py:136
Async XLA Ops:
  0.0 31.2 %copy-start = (f32[272,512]{1,0:T(8,128)S(1)}, f32[272,512]{1,0:T(8,128)}, u32[]{:S(2)}) copy-start(f32[272,512]{1,0:T(8,128)} %constant.13.clone.ts_hbm.ts_ref) | copy-start | bytes 1671172
  0.0 31.2 %copy-start.1 = (f32[272,512]{1,0:T(8,128)S(1)}, f32[272,512]{1,0:T(8,128)}, u32[]{:S(2)}) copy-start(f32[272,512]{1,0:T(8,128)} %constant.12.clone.tc_hbm.tc_ref) | copy-start | bytes 1671172
  0.0 31.2 %copy-start.3 = (bf16[256,512]{1,0:T(8,128)(2,1)S(1)}, bf16[256,512]{1,0:T(8,128)(2,1)}, u32[]{:S(2)}) copy-start(bf16[256,512]{1,0:T(8,128)(2,1)} %constant.17.clone.last_ref) | copy-start | bytes 786436
  0.0 31.2 %copy-start.2 = (bf16[4,256,256]{2,1,0:T(8,128)(2,1)S(1)}, bf16[4,256,256]{2,1,0:T(8,128)(2,1)}, u32[]{:S(2)}) copy-start(bf16[4,256,256]{2,1,0:T(8,128)(2,1)} %constant.16.clone.inv_ref) | copy-start | bytes 1572868

commit v2 on v1

--- a/solution.py
+++ b/solution.py
@@ -62,95 +62,77 @@
 CHUNKS = ((0, 128), (128, 144))
 
 
-def inverse_kernel(z_ref, g_ref, fac_ref, inv_ref, tc_ref, ts_ref, last_ref, out_ref, back, y, sem):
-    j = pl.program_id(0)
-    slot = lax.rem(j, 2)
-
-    def copies(at, which):
-        return [
-            pltpu.make_async_copy(
-                y.at[which, q, :, pl.ds(m * Q, Q)],
-                out_ref.at[pl.ds(q * HALF, HALF), m, at, :],
-                sem.at[which, q * RADIX + m],
+def inner_rows(z_ref, g_ref, inv_ref, tc_ref, ts_ref, back, j, q, start, size):
+    rows = pl.ds(start, size)
+    tr, ti = [], []
+    for r in range(RADIX):
+        lo = r * 2 * Q
+        zr = full(z_ref[q, rows, lo : lo + Q])
+        zi = full(z_ref[q, rows, lo + Q : lo + 2 * Q])
+        gr = full(g_ref[j, rows, lo : lo + Q])
+        gi = full(g_ref[j, rows, lo + Q : lo + 2 * Q])
+        prod = jnp.concatenate([half(gr * zr + gi * zi), half(gr * zi - gi * zr)], axis=1)
+        t = dot(prod, inv_ref[r])
+        tr.append(t[:, :Q])
+        ti.append(t[:, Q:])
+    ar, ai, br, bi = tr[0] + tr[2], ti[0] + ti[2], tr[0] - tr[2], ti[0] - ti[2]
+    cr, ci, dr, di = tr[1] + tr[3], ti[1] + ti[3], tr[1] - tr[3], ti[1] - ti[3]
+    inner = ((ar + cr, ai + ci), (br - di, bi + dr), (ar - cr, ai - ci), (br + di, bi - dr))
+    for m in range(RADIX):
+        lanes = slice(m * Q, (m + 1) * Q)
+        ir, ii = inner[m]
+        tc, ts = tc_ref[rows, lanes], ts_ref[rows, lanes]
+        real = half(ir * tc - ii * ts)
+        imag = half(ii * tc + ir * ts)
+        keep = min(size, HALF - start)
+        back[pl.ds(start, keep), lanes] = real[:keep]
+        back[pl.ds(HALF + start, keep), lanes] = imag[:keep]
+        if start + size == ROWS:
+            top = back[HALF : HALF + 16, lanes]
+            first_row = lax.broadcasted_iota(jnp.int32, (16, Q), 0) == 0
+            back[HALF : HALF + 16, lanes] = half(
+                jnp.where(first_row, full(real[keep : keep + 16]), full(top))
             )
-            for q in range(2)
-            for m in range(RADIX)
-        ]
-
-    @pl.when(j >= 2)
-    def _():
-        for c in copies(j - 2, slot):
-            c.wait()
-
-    factor = fac_ref[0, 0:1, 0:1]
-    for q in range(2):
-        for start, size in CHUNKS:
-            rows = pl.ds(start, size)
-            tr, ti = [], []
-            for r in range(RADIX):
-                lo = r * 2 * Q
-                zr = full(z_ref[q, rows, lo : lo + Q])
-                zi = full(z_ref[q, rows, lo + Q : lo + 2 * Q])
-                gr = full(g_ref[0, rows, lo : lo + Q])
-                gi = full(g_ref[0, rows, lo + Q : lo + 2 * Q])
-                prod = jnp.concatenate([half(gr * zr + gi * zi), half(gr * zi - gi * zr)], axis=1)
-                t = dot(prod, inv_ref[r])
-                tr.append(t[:, :Q])
-                ti.append(t[:, Q:])
-            ar, ai, br, bi = tr[0] + tr[2], ti[0] + ti[2], tr[0] - tr[2], ti[0] - ti[2]
-            cr, ci, dr, di = tr[1] + tr[3], ti[1] + ti[3], tr[1] - tr[3], ti[1] - ti[3]
-            inner = ((ar + cr, ai + ci), (br - di, bi + dr), (ar - cr, ai - ci), (br + di, bi - dr))
-            for m in range(RADIX):
-                lanes = slice(m * Q, (m + 1) * Q)
-                ir, ii = inner[m]
-                tc, ts = tc_ref[rows, lanes], ts_ref[rows, lanes]
-                real = half(ir * tc - ii * ts)
-                imag = half(ii * tc + ir * ts)
-                keep = min(size, HALF - start)
-                back[q, pl.ds(start, keep), lanes] = real[:keep]
-                if start == 0:
-                    back[q, pl.ds(HALF, keep), lanes] = imag[:keep]
-                else:
-                    back[q, pl.ds(HALF + start, keep), lanes] = imag[:keep]
-                    top = back[q, HALF : HALF + 16, lanes]
-                    first_row = lax.broadcasted_iota(jnp.int32, (16, Q), 0) == 0
-                    back[q, HALF : HALF + 16, lanes] = half(
-                        jnp.where(first_row, full(real[keep : keep + 16]), full(top))
-                    )
-        y[slot, q] = dot(last_ref[...], back[q]) * factor
-
-    for c in copies(j, slot):
-        c.start()
-
-    @pl.when(j == pl.num_programs(0) - 1)
-    def _():
-        for c in copies(j - 1, 1 - slot):
-            c.wait()
-        for c in copies(j, slot):
-            c.wait()
+
+
+def inverse_kernel(n, z_ref, g_ref, fac_ref, inv_ref, tc_ref, ts_ref, last_ref, out_ref, back, y, sem):
+    copies = []
+
+    def last_rows(j, q):
+        y[j, q] = dot(last_ref[...], back[j % 2, q]) * fac_ref[j, 0:1, 0:1]
+        for m in range(RADIX):
+            copy = pltpu.make_async_copy(
+                y.at[j, q, :, pl.ds(m * Q, Q)],
+                out_ref.at[pl.ds(q * HALF, HALF), m, j, :],
+                sem.at[j, q * RADIX + m],
+            )
+            copy.start()
+            copies.append(copy)
+
+    steps = [(j, q) for j in range(n) for q in range(2)]
+    for i in range(len(steps) + 1):
+        if i < len(steps):
+            j, q = steps[i]
+            for start, size in CHUNKS:
+                inner_rows(z_ref, g_ref, inv_ref, tc_ref, ts_ref, back.at[j % 2, q], j, q, start, size)
+        if i > 0:
+            last_rows(*steps[i - 1])
+
+    for copy in copies:
+        copy.wait()
 
 
 def inverse(z, g, fac, inv, tc, ts, last):
     n = g.shape[0]
-    whole = lambda *shape: pl.BlockSpec(shape, lambda j: (0,) * len(shape))
     return pl.pallas_call(
-        inverse_kernel,
-        grid=(n,),
-        in_specs=[
-            whole(2, ROWS, 2 * R),
-            pl.BlockSpec((1, ROWS, 2 * R), lambda j: (j, 0, 0)),
-            pl.BlockSpec((1, 8, Q), lambda j: (j, 0, 0)),
-            whole(RADIX, HALF, HALF),
-            whole(ROWS, R),
-            whole(ROWS, R),
-            whole(HALF, R),
-        ],
+        functools.partial(inverse_kernel, n),
+        in_specs=[pl.BlockSpec(memory_space=pltpu.VMEM)] * 7,
         out_specs=pl.BlockSpec(memory_space=pl.ANY),
         out_shape=jax.ShapeDtypeStruct((2 * HALF, RADIX, n, Q), jnp.float32),
         scratch_shapes=[
-            pltpu.VMEM((2, R, R), jnp.bfloat16),
-            pltpu.VMEM((2, 2, HALF, R), jnp.float32),
-            pltpu.SemaphoreType.DMA((2, 2 * RADIX)),
+            pltpu.VMEM((2, 2, R, R), jnp.bfloat16),
+            pltpu.VMEM((n, 2, HALF, R), jnp.float32),
+            pltpu.SemaphoreType.DMA((n, 2 * RADIX)),
         ],
         compiler_params=pltpu.CompilerParams(vmem_limit_bytes=32 << 20),
         name="inverse",
@@ -175,6 +157,44 @@
     ]
 
 
+def torus(t, b):
+    x, y_lo = lax.rem(b, 4), lax.div(b, 4)
+    core, z, y_hi = lax.rem(t, 2), lax.rem(lax.div(t, 2), 4), lax.div(t, 8)
+    y = 2 * y_hi + y_lo
+    x_part = [lax.rem(x + d, 4) for d in range(4)]
+    y_at = [lax.rem(y + d, 4) for d in range(4)]
+    y_bank = [4 * lax.rem(v, 2) for v in y_at]
+    y_tm = [8 * lax.div(v, 2) for v in y_at]
+    z_part = [2 * lax.rem(z + d, 4) for d in range(4)]
+    core_part = [core, 1 - core]
+
+    def at(dx, dy, dz, dc):
+        return {"tm": y_tm[dy] + z_part[dz] + core_part[dc], "bank": y_bank[dy] + x_part[dx]}
+
+    def bank_at(dx, pair):
+        other = lax.rem(y_lo + pair, 2)
+        index = 4 * other + x_part[dx % 4]
+        return index, {"tm": t, "bank": index}
+
+    return at, bank_at
+
+
+HOPS = (0, 1, 2, 1)
+EVERYWHERE = sorted(
+    [
+        (dx, dy, dz, dc)
+        for dx in range(4)
+        for dy in range(4)
+        for dz in range(4)
+        for dc in range(2)
+        if (dx, dy, dz, dc) != (0, 0, 0, 0)
+    ],
+    key=lambda d: -(HOPS[d[0]] + HOPS[d[1]] + HOPS[d[2]]),
+)
+ALONG_TM = [d for d in EVERYWHERE if d[0] == 0 and d[1] in (0, 2)]
+BANK_PEERS = ((2, 1), (1, 1), (-1, 1), (2, 0), (1, 0), (-1, 0), (0, 1))
+
+
 def spectrum_kernel(
     tm, bank, total_blocks,
     strain_ref, lens_hbm, tmpl_hbm, first_hbm, tc_hbm, ts_hbm, fwd_hbm,
@@ -185,9 +205,16 @@
 ):
     t = lax.axis_index("tm")
     b = lax.axis_index("bank")
+    at, bank_at = torus(t, b)
     piece = HALF // bank
     band = HALF // bank
     tiles = band // 8 * RADIX
+
+    barrier = pltpu.get_barrier_semaphore()
+    for d in ALONG_TM:
+        pl.semaphore_signal(barrier, 1, device_id=at(*d), device_id_type=MESH)
+    for dx, pair in BANK_PEERS:
+        pl.semaphore_signal(barrier, 1, device_id=bank_at(dx, pair)[1], device_id_type=MESH)
 
     loads = [(lens_hbm, lens_ref)]
     for c in range(2):
@@ -198,16 +225,6 @@
     for load in loads:
         load.start()
 
-    barrier = pltpu.get_barrier_semaphore()
-    for i in range(1, bank):
-        pl.semaphore_signal(
-            barrier, 1, device_id={"tm": t, "bank": lax.rem(b + i, bank)}, device_id_type=MESH
-        )
-    for i in range(1, tm):
-        pl.semaphore_signal(
-            barrier, 1, device_id={"tm": lax.rem(t + i, tm), "bank": b}, device_id_type=MESH
-        )
-
     for load in loads[: 2 * RADIX + 1]:
         load.wait()
     own_rows = pl.ds(pl.multiple_of(b * piece, piece), piece)
@@ -224,30 +241,24 @@
 
     pl.semaphore_wait(barrier, bank + tm - 2)
 
-    def gather_copy(i):
+    def rows_of(index):
+        return pl.ds(pl.multiple_of(index * piece, piece), piece)
+
+    def gather(i, source, device):
+        part = blocks.at[:, rows_of(source), :]
         return pltpu.make_async_remote_copy(
-            src_ref=blocks.at[:, own_rows, :],
-            dst_ref=blocks.at[:, own_rows, :],
+            src_ref=part,
+            dst_ref=part,
             send_sem=gather_send.at[i],
             recv_sem=gather_recv.at[i],
-            device_id={"tm": t, "bank": lax.rem(b + i, bank)},
+            device_id=device,
             device_id_type=MESH,
         )
 
-    def gather_arrival(i):
-        source = lax.rem(b - i + bank, bank)
-        rows = pl.ds(pl.multiple_of(source * piece, piece), piece)
-        return pltpu.make_async_remote_copy(
-            src_ref=blocks.at[:, rows, :],
-            dst_ref=blocks.at[:, rows, :],
-            send_sem=gather_send.at[i],
-            recv_sem=gather_recv.at[i],
-            device_id={"tm": t, "bank": source},
-            device_id_type=MESH,
-        )
-
-    for i in range(1, bank):
-        gather_copy(i).start()
+    outgoing = [gather(i, b, bank_at(dx, pair)[1]) for i, (dx, pair) in enumerate(BANK_PEERS)]
+    incoming = [gather(i, *bank_at(-dx, pair)) for i, (dx, pair) in enumerate(BANK_PEERS)]
+    for copy in outgoing:
+        copy.start()
 
     for load in loads[2 * RADIX + 1 :]:
         load.wait()
@@ -275,24 +286,25 @@
         fac_ref[j] = jnp.broadcast_to(factor, (8, Q))
         return carry
 
-    lax.fori_loop(0, g_ref.shape[0], join, 0)
-
-    for i in range(1, bank):
-        gather_arrival(i).wait_recv()
-
-    low = pl.ds(pl.multiple_of(b * band, band), band)
+    n = g_ref.shape[0]
+    lax.fori_loop(0, n // 2, join, 0)
+
+    for copy in incoming:
+        copy.wait_recv()
+
+    band_rows = pl.ds(pl.multiple_of(b * band, band), band)
     low_imag = pl.ds(pl.multiple_of(ROWS + b * band, 16), band)
     table = jnp.concatenate(
         [
-            first[low, 0:HALF],
+            first[band_rows, 0:HALF],
             first[HALF:ROWS, 0:HALF],
             first[low_imag, 0:HALF],
             first[ROWS + HALF : 2 * ROWS, 0:HALF],
         ],
         axis=0,
     )
-    band_tc = jnp.concatenate([tc[low, :], tc[HALF:ROWS, :]], axis=0)
-    band_ts = jnp.concatenate([ts[low, :], ts[HALF:ROWS, :]], axis=0)
+    band_tc = jnp.concatenate([tc[band_rows, :], tc[HALF:ROWS, :]], axis=0)
+    band_ts = jnp.concatenate([ts[band_rows, :], ts[HALF:ROWS, :]], axis=0)
     power = [0.0] * RADIX
     height = band + ROWS - HALF
     for c in range(2):
@@ -306,35 +318,25 @@
         axis=0,
     )
     for i in range(tiles):
-        at = i // RADIX * 8
-        send[i, 0:8, :] = power[i % RADIX][at : at + 8]
-        send[i, 8:16, :] = extra
-
-    def sum_copy(i):
-        to = lax.rem(t + i, tm)
+        low = i // RADIX * 8
+        send[i] = half(jnp.concatenate([power[i % RADIX][low : low + 8], extra], axis=0))
+
+    def sum_copy(i, device, slot):
         return pltpu.make_async_remote_copy(
-            src_ref=send.at[to],
-            dst_ref=recv.at[t],
+            src_ref=send.at[slot],
+            dst_ref=recv.at[i],
             send_sem=sum_send.at[i],
             recv_sem=sum_recv.at[i],
-            device_id={"tm": to, "bank": b},
+            device_id=device,
             device_id_type=MESH,
         )
 
-    def sum_arrival(i):
-        source = lax.rem(t - i + tm, tm)
-        return pltpu.make_async_remote_copy(
-            src_ref=send.at[source],
-            dst_ref=recv.at[source],
-            send_sem=sum_send.at[i],
-            recv_sem=sum_recv.at[i],
-            device_id={"tm": source, "bank": b},
-            device_id_type=MESH,
-        )
-
-    for i in range(1, tm):
-        sum_copy(i).start()
-    recv[t] = send[t]
+    sums = []
+    for i, d in enumerate(ALONG_TM):
+        device = at(*d)
+        sums.append(sum_copy(i, device, device["tm"]))
+    for copy in sums:
+        copy.start()
 
     next_copy = pltpu.make_async_remote_copy(
         src_ref=blocks.at[1],
@@ -357,30 +359,26 @@
 
     region(1, blocks[1], blocks[0])
 
-    for i in range(1, tm):
-        sum_arrival(i).wait_recv()
-    total = recv[0]
-    for i in range(1, tm):
-        total = total + recv[i]
+    total = full(send[t])
+    for copy in sums:
+        copy.wait_recv()
+    for i in range(tm - 1):
+        total = total + full(recv[i])
     weight = lax.rsqrt(total * (1.0 / total_blocks) + epsilon)
     me = b * tm + t
     weights[me] = half(weight[0:8])
 
-    def share_copy(to_t, to_b, slot):
-        return pltpu.make_async_remote_copy(
-            src_ref=weights.at[slot],
-            dst_ref=weights.at[slot],
+    for d in EVERYWHERE:
+        pltpu.make_async_remote_copy(
+            src_ref=weights.at[me],
+            dst_ref=weights.at[me],
             send_sem=share_send,
             recv_sem=share_recv,
-            device_id={"tm": to_t, "bank": to_b},
+            device_id=at(*d),
             device_id_type=MESH,
-        )
-
-    def share(i, carry):
-        share_copy(lax.rem(t + lax.div(i, bank), tm), lax.rem(b + lax.rem(i, bank), bank), me).start()
-        return carry
-
-    lax.fori_loop(1, tm * bank, share, 0)
+        ).start()
+
+    lax.fori_loop(n // 2, n, join, 0)
 
     @pl.when(t > 0)
     def _():
@@ -401,8 +399,8 @@
     def whiten(i, carry):
         rows = pl.ds(pl.multiple_of(i * 16, 16), 16)
         for r in range(RADIX):
-            at = 2 * i * RADIX + r
-            w = jnp.concatenate([full(weights[at]), full(weights[at + RADIX])], axis=0)
+            tile = 2 * i * RADIX + r
+            w = jnp.concatenate([full(weights[tile]), full(weights[tile + RADIX])], axis=0)
             for q in range(2):
                 for p in range(2):
                     lanes = fill_slot(2 * r + p, Q)
@@ -418,10 +416,10 @@
                     zraw[q, HALF:ROWS, lanes] * weight[8 + r : 9 + r]
                 )
 
-    for i in range(1, bank):
-        gather_copy(i).wait_send()
-    for i in range(1, tm):
-        sum_copy(i).wait_send()
+    for copy in outgoing:
+        copy.wait_send()
+    for copy in sums:
+        copy.wait_send()
 
     @pl.when(t < tm - 1)
     def _():
@@ -459,12 +457,12 @@
             pltpu.VMEM((ROWS, R), f32),
             pltpu.VMEM((RADIX, HALF, HALF), bf),
             pltpu.VMEM((2, ROWS, 2 * R), f32),
-            pltpu.VMEM((tm, 16, Q), f32),
-            pltpu.VMEM((tm, 16, Q), f32),
+            pltpu.VMEM((tm, 16, Q), bf),
+            pltpu.VMEM((tm - 1, 16, Q), bf),
             pltpu.VMEM((tm * bank, 8, Q), bf),
             sem((2 * RADIX + 6,)),
-            sem((bank,)),
-            sem((bank,)),
+            sem((bank - 1,)),
+            sem((bank - 1,)),
             sem((tm,)),
             sem((tm,)),
             sem,

time: 38 us -> 35.7 us (0.939)
  Pallas kernels: 37.9 us -> 35.5 us
    pallas_call x1, Pallas kernels: 31.2 us -> 29.8 us  [spectra(): pl.pallas_call(functools.partial(spectrum_kernel, tm, bank, 2 * tm), in_s...]
    pallas_call x1, Pallas kernels: 6.68 us -> 5.72 us  [inverse(): pl.pallas_call(functools.partial(inverse_kernel, n), in_specs=[pl.BlockSp...]
where the time goes in v2:
time: 35.7 us; the launch traced here: 35.6 us
  Pallas kernels  35.5 us (99%)
    pallas_call x1, Pallas kernels, spectra(): pl.pallas_call(functools.partial(spectrum_kernel, tm, bank, 2 * tm), in_s...  29.8 us
    pallas_call x1, Pallas kernels, inverse(): pl.pallas_call(functools.partial(inverse_kernel, n), in_specs=[pl.BlockSp...  5.72 us

profile of v2, /device:TPU:1, one launch (start us, length us, event | category | flops | bytes accessed | tf_op | source)
XLA Modules:
  0.0 35.6 jit_solution(17638579506364105052)
XLA Ops:
  0.0 0.0 copy-start
  0.0 0.0 copy-start.1
  0.0 0.0 copy-start.3
  0.0 0.0 copy-start.2
  0.0 29.8 %spectra.1 = (bf16[2,272,1024]{2,1,0:T(8,128)(2,1)S(1)}, bf16[4,272,1024]{2,1,0:T(8,128)(2,1)S(1)}, f32[4,8,128]{2,1,0:T(8,128)S(1)}) custom-call(f32[32,4,2,128]{3,2,1,0:T(2,128)} %bitcast.10, s32[2]{0:T(128)} %lens_hbm.1, bf16[2,4,512,512]{3,2,1,0:T(8,128)(2,1)} %tmpl_hbm.1, bf16[544,512]{1,0:T(8,128)(2,1)} %constant.14.clone.first_hbm, ...), custom_call_target="tpu_custom_call" | custom-call | tf_op jit(solution)/shard_map/spectra/pallas_call | solution.py:440
  29.9 0.0 copy-done
  29.9 0.0 copy-done.1
  29.9 0.0 copy-done.3
  29.9 0.0 copy-done.2
  29.9 5.7 %inverse.1 = f32[512,4,4,128]{3,2,1,0:T(4,128)} custom-call(bf16[2,272,1024]{2,1,0:T(8,128)(2,1)S(1)} %get-tuple-element.8.z_ref, bf16[4,272,1024]{2,1,0:T(8,128)(2,1)S(1)} %get-tuple-element.9.g_ref, f32[4,8,128]{2,1,0:T(8,128)S(1)} %get-tuple-element.10.fac_ref, bf16[4,256,256]{2,1,0:T(8,128)(2,1)S(1)} %copy-done.2, f32[272,512]{1,0:T(8,128)S(1)} %copy-done.1, ...), custom_call_target="tpu_custom_call" | custom-call | tf_op jit(solution)/shard_map/inverse/pallas_call | solution.py:127
Async XLA Ops:
  0.0 29.9 %copy-start = (f32[272,512]{1,0:T(8,128)S(1)}, f32[272,512]{1,0:T(8,128)}, u32[]{:S(2)}) copy-start(f32[272,512]{1,0:T(8,128)} %constant.13.clone.ts_hbm.ts_ref) | copy-start | bytes 1671172
  0.0 29.9 %copy-start.1 = (f32[272,512]{1,0:T(8,128)S(1)}, f32[272,512]{1,0:T(8,128)}, u32[]{:S(2)}) copy-start(f32[272,512]{1,0:T(8,128)} %constant.12.clone.tc_hbm.tc_ref) | copy-start | bytes 1671172
  0.0 29.9 %copy-start.3 = (bf16[256,512]{1,0:T(8,128)(2,1)S(1)}, bf16[256,512]{1,0:T(8,128)(2,1)}, u32[]{:S(2)}) copy-start(bf16[256,512]{1,0:T(8,128)(2,1)} %constant.17.clone.last_ref) | copy-start | bytes 786436
  0.0 29.9 %copy-start.2 = (bf16[4,256,256]{2,1,0:T(8,128)(2,1)S(1)}, bf16[4,256,256]{2,1,0:T(8,128)(2,1)}, u32[]{:S(2)}) copy-start(bf16[4,256,256]{2,1,0:T(8,128)(2,1)} %constant.16.clone.inv_ref) | copy-start | bytes 1572868

commit v3 on v2

--- a/solution.py
+++ b/solution.py
@@ -59,7 +59,7 @@
     return jnp.dot(a, b, preferred_element_type=jnp.float32)
 
 
-CHUNKS = ((0, 128), (128, 144))
+CHUNKS = ((0, 272),)
 
 
 def inner_rows(z_ref, g_ref, inv_ref, tc_ref, ts_ref, back, j, q, start, size):
@@ -67,11 +67,11 @@
     tr, ti = [], []
     for r in range(RADIX):
         lo = r * 2 * Q
-        zr = full(z_ref[q, rows, lo : lo + Q])
-        zi = full(z_ref[q, rows, lo + Q : lo + 2 * Q])
-        gr = full(g_ref[j, rows, lo : lo + Q])
-        gi = full(g_ref[j, rows, lo + Q : lo + 2 * Q])
-        prod = jnp.concatenate([half(gr * zr + gi * zi), half(gr * zi - gi * zr)], axis=1)
+        zr = z_ref[q, rows, lo : lo + Q]
+        zi = z_ref[q, rows, lo + Q : lo + 2 * Q]
+        gr = g_ref[j, rows, lo : lo + Q]
+        gi = g_ref[j, rows, lo + Q : lo + 2 * Q]
+        prod = jnp.concatenate([gr * zr + gi * zi, gr * zi - gi * zr], axis=1)
         t = dot(prod, inv_ref[r])
         tr.append(t[:, :Q])
         ti.append(t[:, Q:])
@@ -80,10 +80,10 @@
     inner = ((ar + cr, ai + ci), (br - di, bi + dr), (ar - cr, ai - ci), (br + di, bi - dr))
     for m in range(RADIX):
         lanes = slice(m * Q, (m + 1) * Q)
-        ir, ii = inner[m]
+        ir, ii = half(inner[m][0]), half(inner[m][1])
         tc, ts = tc_ref[rows, lanes], ts_ref[rows, lanes]
-        real = half(ir * tc - ii * ts)
-        imag = half(ii * tc + ir * ts)
+        real = ir * tc - ii * ts
+        imag = ii * tc + ir * ts
         keep = min(size, HALF - start)
         back[pl.ds(start, keep), lanes] = real[:keep]
         back[pl.ds(HALF + start, keep), lanes] = imag[:keep]
@@ -95,11 +95,11 @@
             )
 
 
-def inverse_kernel(n, z_ref, g_ref, fac_ref, inv_ref, tc_ref, ts_ref, last_ref, out_ref, back, y, sem):
+def inverse_kernel(n, z_ref, g_ref, inv_ref, tc_ref, ts_ref, last_ref, out_ref, back, y, sem):
     copies = []
 
     def last_rows(j, q):
-        y[j, q] = dot(last_ref[...], back[j % 2, q]) * fac_ref[j, 0:1, 0:1]
+        y[j, q] = dot(last_ref[...], back[j % 2, q])
         for m in range(RADIX):
             copy = pltpu.make_async_copy(
                 y.at[j, q, :, pl.ds(m * Q, Q)],
@@ -122,11 +122,11 @@
         copy.wait()
 
 
-def inverse(z, g, fac, inv, tc, ts, last):
+def inverse(z, g, inv, tc, ts, last):
     n = g.shape[0]
     return pl.pallas_call(
         functools.partial(inverse_kernel, n),
-        in_specs=[pl.BlockSpec(memory_space=pltpu.VMEM)] * 7,
+        in_specs=[pl.BlockSpec(memory_space=pltpu.VMEM)] * 6,
         out_specs=pl.BlockSpec(memory_space=pl.ANY),
         out_shape=jax.ShapeDtypeStruct((2 * HALF, RADIX, n, Q), jnp.float32),
         scratch_shapes=[
@@ -136,7 +136,7 @@
         ],
         compiler_params=pltpu.CompilerParams(vmem_limit_bytes=32 << 20),
         name="inverse",
-    )(z, g, fac, inv, tc, ts, last)
+    )(z, g, inv, tc, ts, last)
 
 
 def fill_slot(i, lanes):
@@ -176,7 +176,11 @@
         index = 4 * other + x_part[dx % 4]
         return index, {"tm": t, "bank": index}
 
-    return at, bank_at
+    def same_half(dx, pair, dz, dc):
+        other = lax.rem(y_lo + pair, 2)
+        return {"tm": 8 * y_hi + z_part[dz] + core_part[dc], "bank": 4 * other + x_part[dx]}
+
+    return at, bank_at, same_half
 
 
 HOPS = (0, 1, 2, 1)
@@ -191,6 +195,17 @@
     ],
     key=lambda d: -(HOPS[d[0]] + HOPS[d[1]] + HOPS[d[2]]),
 )
+NEARER_HALF = sorted(
+    [
+        (dx, pair, dz, dc)
+        for dx in range(4)
+        for pair in range(2)
+        for dz in range(4)
+        for dc in range(2)
+        if (dx, pair, dz, dc) != (0, 0, 0, 0)
+    ],
+    key=lambda d: -(HOPS[d[0]] + d[1] + HOPS[d[2]]),
+)
 ALONG_TM = [d for d in EVERYWHERE if d[0] == 0 and d[1] in (0, 2)]
 BANK_PEERS = ((2, 1), (1, 1), (-1, 1), (2, 0), (1, 0), (-1, 0), (0, 1))
 
@@ -198,17 +213,20 @@
 def spectrum_kernel(
     tm, bank, total_blocks,
     strain_ref, lens_hbm, tmpl_hbm, first_hbm, tc_hbm, ts_hbm, fwd_hbm,
-    z_ref, g_ref, fac_ref,
+    z_ref, g_ref, tc_ref, ts_ref,
     lens_ref, raw, blocks, prev, tmpl, first, tc, ts, fwd, zraw, send, recv, weights,
     load_sem, gather_send, gather_recv, sum_send, sum_recv, prev_send, prev_recv,
     share_send, share_recv,
 ):
     t = lax.axis_index("tm")
     b = lax.axis_index("bank")
-    at, bank_at = torus(t, b)
+    at, bank_at, same_half = torus(t, b)
     piece = HALF // bank
     band = HALF // bank
     tiles = band // 8 * RADIX
+    owners = tm // 2
+    per = tiles // owners
+    own = lax.rem(t, owners)
 
     barrier = pltpu.get_barrier_semaphore()
     for d in ALONG_TM:
@@ -262,6 +280,8 @@
 
     for load in loads[2 * RADIX + 1 :]:
         load.wait()
+    tc_ref[...] = half(tc[...])
+    ts_ref[...] = half(ts[...])
     row = lax.broadcasted_iota(jnp.int32, (R, R), 0)
     col = lax.broadcasted_iota(jnp.int32, (R, R), 1)
     order = lax.rem(col, Q) * RADIX + lax.div(col, Q)
@@ -274,16 +294,16 @@
     def join(j, carry):
         norm = jnp.zeros((1, R), jnp.float32)
         for p in range(2):
+            values = full(tmpl[p, j])
+            norm = norm + jnp.sum(values * values, axis=0, keepdims=True)
+        factor = lax.rsqrt(jnp.sum(norm, axis=1, keepdims=True))
+        for p in range(2):
             direct = dot(tmpl[p, j, 0:ROWS, :], pick)
             mirror = dot(flip, half(dot(tmpl[p, j, HALF:R, :], pick_mirror)))
-            joined = half(direct + mirror if p == 0 else direct - mirror)
+            joined = half((direct + mirror if p == 0 else direct - mirror) * factor)
             for r in range(RADIX):
                 lo = (2 * r + p) * Q
                 g_ref[j, :, lo : lo + Q] = joined[:, fill_slot(r, Q)]
-            values = full(tmpl[p, j])
-            norm = norm + jnp.sum(values * values, axis=0, keepdims=True)
-        factor = lax.rsqrt(jnp.sum(norm, axis=1, keepdims=True))
-        fac_ref[j] = jnp.broadcast_to(factor, (8, Q))
         return carry
 
     n = g_ref.shape[0]
@@ -317,9 +337,13 @@
         [power[r][band : band + 1] for r in range(RADIX)] + [jnp.zeros((8 - RADIX, Q), jnp.float32)],
         axis=0,
     )
-    for i in range(tiles):
-        low = i // RADIX * 8
-        send[i] = half(jnp.concatenate([power[i % RADIX][low : low + 8], extra], axis=0))
+    for o in range(owners):
+        parts = []
+        for i in range(o * per, (o + 1) * per):
+            low = i // RADIX * 8
+            parts.append(power[i % RADIX][low : low + 8])
+        parts += [extra, jnp.zeros((8, Q), jnp.float32)]
+        send[o] = half(jnp.concatenate(parts, axis=0))
 
     def sum_copy(i, device, slot):
         return pltpu.make_async_remote_copy(
@@ -334,7 +358,7 @@
     sums = []
     for i, d in enumerate(ALONG_TM):
         device = at(*d)
-        sums.append(sum_copy(i, device, device["tm"]))
+        sums.append(sum_copy(i, device, lax.rem(device["tm"], owners)))
     for copy in sums:
         copy.start()
 
@@ -359,22 +383,23 @@
 
     region(1, blocks[1], blocks[0])
 
-    total = full(send[t])
+    total = full(send[own])
     for copy in sums:
         copy.wait_recv()
     for i in range(tm - 1):
         total = total + full(recv[i])
     weight = lax.rsqrt(total * (1.0 / total_blocks) + epsilon)
-    me = b * tm + t
-    weights[me] = half(weight[0:8])
-
-    for d in EVERYWHERE:
+    mine = pl.ds(b * tiles + own * per, per)
+    for i in range(per):
+        weights[b * tiles + own * per + i] = half(weight[8 * i : 8 * i + 8])
+
+    for d in NEARER_HALF:
         pltpu.make_async_remote_copy(
-            src_ref=weights.at[me],
-            dst_ref=weights.at[me],
+            src_ref=weights.at[mine],
+            dst_ref=weights.at[mine],
             send_sem=share_send,
             recv_sem=share_recv,
-            device_id=at(*d),
+            device_id=same_half(*d),
             device_id_type=MESH,
         ).start()
 
@@ -387,8 +412,8 @@
     region(0, blocks[0], prev[...])
 
     others = pltpu.make_async_remote_copy(
-        src_ref=weights.at[pl.ds(0, tm * bank - 1)],
-        dst_ref=weights.at[pl.ds(0, tm * bank - 1)],
+        src_ref=weights.at[pl.ds(0, tiles * bank - per)],
+        dst_ref=weights.at[pl.ds(0, tiles * bank - per)],
         send_sem=share_send,
         recv_sem=share_recv,
         device_id={"tm": t, "bank": lax.rem(b + 1, bank)},
@@ -413,7 +438,7 @@
             for p in range(2):
                 lanes = fill_slot(2 * r + p, Q)
                 z_ref[q, HALF:ROWS, lanes] = half(
-                    zraw[q, HALF:ROWS, lanes] * weight[8 + r : 9 + r]
+                    zraw[q, HALF:ROWS, lanes] * weight[8 * per + r : 8 * per + r + 1]
                 )
 
     for copy in outgoing:
@@ -440,11 +465,12 @@
     return pl.pallas_call(
         functools.partial(spectrum_kernel, tm, bank, 2 * tm),
         in_specs=[hbm] * 7,
-        out_specs=[vmem] * 3,
+        out_specs=[vmem] * 4,
         out_shape=[
             jax.ShapeDtypeStruct((2, ROWS, 2 * R), bf),
             jax.ShapeDtypeStruct((n, ROWS, 2 * R), bf),
-            jax.ShapeDtypeStruct((n, 8, Q), f32),
+            jax.ShapeDtypeStruct((ROWS, R), bf),
+            jax.ShapeDtypeStruct((ROWS, R), bf),
         ],
         scratch_shapes=[
             pltpu.SMEM((2,), jnp.int32),
@@ -457,9 +483,9 @@
             pltpu.VMEM((ROWS, R), f32),
             pltpu.VMEM((RADIX, HALF, HALF), bf),
             pltpu.VMEM((2, ROWS, 2 * R), f32),
-            pltpu.VMEM((tm, 16, Q), bf),
-            pltpu.VMEM((tm - 1, 16, Q), bf),
-            pltpu.VMEM((tm * bank, 8, Q), bf),
+            pltpu.VMEM((tm // 2, 32, Q), bf),
+            pltpu.VMEM((tm - 1, 32, Q), bf),
+            pltpu.VMEM((HALF // 8 * RADIX, 8, Q), bf),
             sem((2 * RADIX + 6,)),
             sem((bank - 1,)),
             sem((bank - 1,)),
@@ -482,8 +508,8 @@
     bf = lambda x: jnp.asarray(x, jnp.bfloat16)
     f32 = lambda x: jnp.asarray(x, jnp.float32)
     tc, ts = f32(tc), f32(ts)
-    z, g, fac = spectra(strain, lengths, templates, (bf(first), tc, ts, bf(fwd)), tm, bank)
-    out = inverse(z, g, fac, bf(inv), tc, ts, bf(last))
+    z, g, tc16, ts16 = spectra(strain, lengths, templates, (bf(first), tc, ts, bf(fwd)), tm, bank)
+    out = inverse(z, g, bf(inv), tc16, ts16, bf(last))
     n = templates.shape[1]
     return out.reshape(2 * HALF * RADIX, n, Q).transpose(1, 0, 2).reshape(n, 2 * HALF * R)
 

time: 35.7 us -> 34.1 us (0.955)
  Pallas kernels: 35.5 us -> 34 us
    pallas_call x1, Pallas kernels: 29.8 us -> 28.6 us  [spectra(): pl.pallas_call(functools.partial(spectrum_kernel, tm, bank, 2 * tm), in_s...]
where the time goes in v3:
time: 34.1 us; the launch traced here: 34 us
  Pallas kernels  34 us (100%)
    pallas_call x1, Pallas kernels, spectra(): pl.pallas_call(functools.partial(spectrum_kernel, tm, bank, 2 * tm), in_s...  28.6 us
    pallas_call x1, Pallas kernels, inverse(): pl.pallas_call(functools.partial(inverse_kernel, n), in_specs=[pl.BlockSp...  5.39 us

profile of v3, /device:TPU:1, one launch (start us, length us, event | category | flops | bytes accessed | tf_op | source)
XLA Modules:
  0.0 34.0 jit_solution(8478584773174298429)
XLA Ops:
  0.0 0.0 copy-start.1
  0.0 0.0 copy-start
  0.0 28.6 %spectra.1 = (bf16[2,272,1024]{2,1,0:T(8,128)(2,1)S(1)}, bf16[4,272,1024]{2,1,0:T(8,128)(2,1)S(1)}, bf16[272,512]{1,0:T(8,128)(2,1)S(1)}, bf16[272,512]{1,0:T(8,128)(2,1)S(1)}) custom-call(f32[32,4,2,128]{3,2,1,0:T(2,128)} %bitcast.10, s32[2]{0:T(128)} %lens_hbm.1, bf16[2,4,512,512]{3,2,1,0:T(8,128)(2,1)} %tmpl_hbm.1, ...), custom_call_target="tpu_custom_call" | custom-call | tf_op jit(solution)/shard_map/spectra/pallas_call | solution.py:465
  28.6 0.0 copy-done.1
  28.6 0.0 copy-done
  28.6 5.4 %inverse.1 = f32[512,4,4,128]{3,2,1,0:T(4,128)} custom-call(bf16[2,272,1024]{2,1,0:T(8,128)(2,1)S(1)} %get-tuple-element.9.z_ref, bf16[4,272,1024]{2,1,0:T(8,128)(2,1)S(1)} %get-tuple-element.10.g_ref, bf16[4,256,256]{2,1,0:T(8,128)(2,1)S(1)} %copy-done, bf16[272,512]{1,0:T(8,128)(2,1)S(1)} %get-tuple-element.11.tc_ref, ...), custom_call_target="tpu_custom_call" | custom-call | tf_op jit(solution)/shard_map/inverse/pallas_call | solution.py:127
Async XLA Ops:
  0.0 28.6 %copy-start.1 = (bf16[256,512]{1,0:T(8,128)(2,1)S(1)}, bf16[256,512]{1,0:T(8,128)(2,1)}, u32[]{:S(2)}) copy-start(bf16[256,512]{1,0:T(8,128)(2,1)} %constant.17.clone.last_ref) | copy-start | bytes 786436
  0.0 28.6 %copy-start = (bf16[4,256,256]{2,1,0:T(8,128)(2,1)S(1)}, bf16[4,256,256]{2,1,0:T(8,128)(2,1)}, u32[]{:S(2)}) copy-start(bf16[4,256,256]{2,1,0:T(8,128)(2,1)} %constant.16.clone.inv_ref) | copy-start | bytes 1572868

commit v4 on v3

--- a/solution.py
+++ b/solution.py
@@ -206,6 +206,7 @@
     ],
     key=lambda d: -(HOPS[d[0]] + d[1] + HOPS[d[2]]),
 )
+NEXT_ALONG_TM = ((0, 0, 1, 0), (0, 0, 3, 0), (0, 2, 0, 0), (0, 0, 0, 1))
 ALONG_TM = [d for d in EVERYWHERE if d[0] == 0 and d[1] in (0, 2)]
 BANK_PEERS = ((2, 1), (1, 1), (-1, 1), (2, 0), (1, 0), (-1, 0), (0, 1))
 
@@ -216,7 +217,7 @@
     z_ref, g_ref, tc_ref, ts_ref,
     lens_ref, raw, blocks, prev, tmpl, first, tc, ts, fwd, zraw, send, recv, weights,
     load_sem, gather_send, gather_recv, sum_send, sum_recv, prev_send, prev_recv,
-    share_send, share_recv,
+    share_send, share_recv, word,
 ):
     t = lax.axis_index("tm")
     b = lax.axis_index("bank")
@@ -228,19 +229,22 @@
     per = tiles // owners
     own = lax.rem(t, owners)
 
-    barrier = pltpu.get_barrier_semaphore()
-    for d in ALONG_TM:
-        pl.semaphore_signal(barrier, 1, device_id=at(*d), device_id_type=MESH)
-    for dx, pair in BANK_PEERS:
-        pl.semaphore_signal(barrier, 1, device_id=bank_at(dx, pair)[1], device_id_type=MESH)
-
     loads = [(lens_hbm, lens_ref)]
     for c in range(2):
         for m in range(RADIX):
             loads.append((strain_ref.at[:, m, c, :], raw.at[c, :, pl.ds(m * Q, Q)]))
     loads += [(first_hbm, first), (tc_hbm, tc), (ts_hbm, ts), (fwd_hbm, fwd), (tmpl_hbm, tmpl)]
     loads = [pltpu.make_async_copy(s, d, load_sem.at[i]) for i, (s, d) in enumerate(loads)]
-    for load in loads:
+    for load in loads[: 2 * RADIX + 1]:
+        load.start()
+
+    barrier = pltpu.get_barrier_semaphore()
+    for dx, pair in BANK_PEERS:
+        pl.semaphore_signal(barrier, 1, device_id=bank_at(dx, pair)[1], device_id_type=MESH)
+    for d in NEXT_ALONG_TM:
+        pl.semaphore_signal(barrier, 1, device_id=at(*d), device_id_type=MESH)
+
+    for load in loads[2 * RADIX + 1 :]:
         load.start()
 
     for load in loads[: 2 * RADIX + 1]:
@@ -257,7 +261,7 @@
     def _():
         prev[...] = jnp.zeros_like(prev)
 
-    pl.semaphore_wait(barrier, bank + tm - 2)
+    pl.semaphore_wait(barrier, bank - 1 + len(NEXT_ALONG_TM))
 
     def rows_of(index):
         return pl.ds(pl.multiple_of(index * piece, piece), piece)
@@ -277,6 +281,15 @@
     incoming = [gather(i, *bank_at(-dx, pair)) for i, (dx, pair) in enumerate(BANK_PEERS)]
     for copy in outgoing:
         copy.start()
+
+    def tell(i):
+        for d in NEXT_ALONG_TM:
+            pl.semaphore_signal(word.at[i], 1, device_id=at(*d), device_id_type=MESH)
+
+    def hear(i):
+        pl.semaphore_wait(word.at[i], len(NEXT_ALONG_TM))
+
+    tell(0)
 
     for load in loads[2 * RADIX + 1 :]:
         load.wait()
@@ -307,7 +320,12 @@
         return carry
 
     n = g_ref.shape[0]
-    lax.fori_loop(0, n // 2, join, 0)
+    lax.fori_loop(0, 1, join, 0)
+    hear(0)
+    tell(1)
+    lax.fori_loop(1, n // 2, join, 0)
+    hear(1)
+    tell(2)
 
     for copy in incoming:
         copy.wait_recv()
@@ -359,6 +377,7 @@
     for i, d in enumerate(ALONG_TM):
         device = at(*d)
         sums.append(sum_copy(i, device, lax.rem(device["tm"], owners)))
+    hear(2)
     for copy in sums:
         copy.start()
 
@@ -495,6 +514,7 @@
             sem,
             sem,
             sem,
+            pltpu.SemaphoreType.REGULAR((3,)),
         ],
         compiler_params=pltpu.CompilerParams(
             collective_id=0, has_side_effects=True, vmem_limit_bytes=32 << 20

time: 34.1 us -> 33.3 us (0.977)
  Pallas kernels: 34 us -> 33.1 us
    pallas_call x1, Pallas kernels: 28.6 us -> 27.7 us  [spectra(): pl.pallas_call(functools.partial(spectrum_kernel, tm, bank, 2 * tm), in_s...]
where the time goes in v4:
time: 33.3 us; the launch traced here: 33.2 us
  Pallas kernels  33.1 us (99%)
    pallas_call x1, Pallas kernels, spectra(): pl.pallas_call(functools.partial(spectrum_kernel, tm, bank, 2 * tm), in_s...  27.7 us
    pallas_call x1, Pallas kernels, inverse(): pl.pallas_call(functools.partial(inverse_kernel, n), in_specs=[pl.BlockSp...  5.39 us

profile of v4, /device:TPU:1, one launch (start us, length us, event | category | flops | bytes accessed | tf_op | source)
XLA Modules:
  0.0 33.2 jit_solution(5437013354563099412)
XLA Ops:
  0.0 0.0 copy-start.1
  0.0 0.0 copy-start
  0.0 27.7 %spectra.1 = (bf16[2,272,1024]{2,1,0:T(8,128)(2,1)S(1)}, bf16[4,272,1024]{2,1,0:T(8,128)(2,1)S(1)}, bf16[272,512]{1,0:T(8,128)(2,1)S(1)}, bf16[272,512]{1,0:T(8,128)(2,1)S(1)}) custom-call(f32[32,4,2,128]{3,2,1,0:T(2,128)} %bitcast.10, s32[2]{0:T(128)} %lens_hbm.1, bf16[2,4,512,512]{3,2,1,0:T(8,128)(2,1)} %tmpl_hbm.1, ...), custom_call_target="tpu_custom_call" | custom-call | tf_op jit(solution)/shard_map/spectra/pallas_call | solution.py:484
  27.8 0.0 copy-done.1
  27.8 0.0 copy-done
  27.8 5.4 %inverse.1 = f32[512,4,4,128]{3,2,1,0:T(4,128)} custom-call(bf16[2,272,1024]{2,1,0:T(8,128)(2,1)S(1)} %get-tuple-element.9.z_ref, bf16[4,272,1024]{2,1,0:T(8,128)(2,1)S(1)} %get-tuple-element.10.g_ref, bf16[4,256,256]{2,1,0:T(8,128)(2,1)S(1)} %copy-done, bf16[272,512]{1,0:T(8,128)(2,1)S(1)} %get-tuple-element.11.tc_ref, ...), custom_call_target="tpu_custom_call" | custom-call | tf_op jit(solution)/shard_map/inverse/pallas_call | solution.py:127
Async XLA Ops:
  0.0 27.8 %copy-start.1 = (bf16[256,512]{1,0:T(8,128)(2,1)S(1)}, bf16[256,512]{1,0:T(8,128)(2,1)}, u32[]{:S(2)}) copy-start(bf16[256,512]{1,0:T(8,128)(2,1)} %constant.17.clone.last_ref) | copy-start | bytes 786436
  0.0 27.8 %copy-start = (bf16[4,256,256]{2,1,0:T(8,128)(2,1)S(1)}, bf16[4,256,256]{2,1,0:T(8,128)(2,1)}, u32[]{:S(2)}) copy-start(bf16[4,256,256]{2,1,0:T(8,128)(2,1)} %constant.16.clone.inv_ref) | copy-start | bytes 1572868

commit v5 on v4

--- a/solution.py
+++ b/solution.py
@@ -99,11 +99,14 @@
     copies = []
 
     def last_rows(j, q):
-        y[j, q] = dot(last_ref[...], back[j % 2, q])
+        y[j, pl.ds(q * HALF, HALF)] = dot(last_ref[...], back[j % 2, q])
+        if q == 0 and j < n - 1:
+            return
+        at, size = (0, 2 * HALF) if j < n - 1 else (q * HALF, HALF)
         for m in range(RADIX):
             copy = pltpu.make_async_copy(
-                y.at[j, q, :, pl.ds(m * Q, Q)],
-                out_ref.at[pl.ds(q * HALF, HALF), m, j, :],
+                y.at[j, pl.ds(at, size), pl.ds(m * Q, Q)],
+                out_ref.at[pl.ds(at, size), m, j, :],
                 sem.at[j, q * RADIX + m],
             )
             copy.start()
@@ -131,7 +134,7 @@
         out_shape=jax.ShapeDtypeStruct((2 * HALF, RADIX, n, Q), jnp.float32),
         scratch_shapes=[
             pltpu.VMEM((2, 2, R, R), jnp.bfloat16),
-            pltpu.VMEM((n, 2, HALF, R), jnp.float32),
+            pltpu.VMEM((n, 2 * HALF, R), jnp.float32),
             pltpu.SemaphoreType.DMA((n, 2 * RADIX)),
         ],
         compiler_params=pltpu.CompilerParams(vmem_limit_bytes=32 << 20),

time: 33.3 us -> 33 us (level)
  no operation moved by 1% of the time
where the time goes in v5:
time: 33 us; the launch traced here: 32.9 us
  Pallas kernels  32.8 us (99%)
    pallas_call x1, Pallas kernels, spectra(): pl.pallas_call(functools.partial(spectrum_kernel, tm, bank, 2 * tm), in_s...  27.7 us
    pallas_call x1, Pallas kernels, inverse(): pl.pallas_call(functools.partial(inverse_kernel, n), in_specs=[pl.BlockSp...  5.09 us

profile of v5, /device:TPU:1, one launch (start us, length us, event | category | flops | bytes accessed | tf_op | source)
XLA Modules:
  0.0 32.9 jit_solution(17689039838002505360)
XLA Ops:
  0.0 0.0 copy-start.1
  0.0 0.0 copy-start
  0.0 27.7 %spectra.1 = (bf16[2,272,1024]{2,1,0:T(8,128)(2,1)S(1)}, bf16[4,272,1024]{2,1,0:T(8,128)(2,1)S(1)}, bf16[272,512]{1,0:T(8,128)(2,1)S(1)}, bf16[272,512]{1,0:T(8,128)(2,1)S(1)}) custom-call(f32[32,4,2,128]{3,2,1,0:T(2,128)} %bitcast.10, s32[2]{0:T(128)} %lens_hbm.1, bf16[2,4,512,512]{3,2,1,0:T(8,128)(2,1)} %tmpl_hbm.1, ...), custom_call_target="tpu_custom_call" | custom-call | tf_op jit(solution)/shard_map/spectra/pallas_call | solution.py:487
  27.8 0.0 copy-done.1
  27.8 0.0 copy-done
  27.8 5.1 %inverse.1 = f32[512,4,4,128]{3,2,1,0:T(4,128)} custom-call(bf16[2,272,1024]{2,1,0:T(8,128)(2,1)S(1)} %get-tuple-element.9.z_ref, bf16[4,272,1024]{2,1,0:T(8,128)(2,1)S(1)} %get-tuple-element.10.g_ref, bf16[4,256,256]{2,1,0:T(8,128)(2,1)S(1)} %copy-done, bf16[272,512]{1,0:T(8,128)(2,1)S(1)} %get-tuple-element.11.tc_ref, ...), custom_call_target="tpu_custom_call" | custom-call | tf_op jit(solution)/shard_map/inverse/pallas_call | solution.py:130
Async XLA Ops:
  0.0 27.8 %copy-start.1 = (bf16[256,512]{1,0:T(8,128)(2,1)S(1)}, bf16[256,512]{1,0:T(8,128)(2,1)}, u32[]{:S(2)}) copy-start(bf16[256,512]{1,0:T(8,128)(2,1)} %constant.17.clone.last_ref) | copy-start | bytes 786436
  0.0 27.8 %copy-start = (bf16[4,256,256]{2,1,0:T(8,128)(2,1)S(1)}, bf16[4,256,256]{2,1,0:T(8,128)(2,1)}, u32[]{:S(2)}) copy-start(bf16[4,256,256]{2,1,0:T(8,128)(2,1)} %constant.16.clone.inv_ref) | copy-start | bytes 1572868

commit v6 on v5

--- a/solution.py
+++ b/solution.py
@@ -222,6 +222,15 @@
     load_sem, gather_send, gather_recv, sum_send, sum_recv, prev_send, prev_recv,
     share_send, share_recv, word,
 ):
+    loads = [(lens_hbm, lens_ref)]
+    for c in range(2):
+        for m in range(RADIX):
+            loads.append((strain_ref.at[:, m, c, :], raw.at[c, :, pl.ds(m * Q, Q)]))
+    loads += [(first_hbm, first), (tc_hbm, tc), (ts_hbm, ts), (fwd_hbm, fwd), (tmpl_hbm, tmpl)]
+    loads = [pltpu.make_async_copy(s, d, load_sem.at[i]) for i, (s, d) in enumerate(loads)]
+    for load in loads[: 2 * RADIX + 1]:
+        load.start()
+
     t = lax.axis_index("tm")
     b = lax.axis_index("bank")
     at, bank_at, same_half = torus(t, b)
@@ -231,15 +240,6 @@
     owners = tm // 2
     per = tiles // owners
     own = lax.rem(t, owners)
-
-    loads = [(lens_hbm, lens_ref)]
-    for c in range(2):
-        for m in range(RADIX):
-            loads.append((strain_ref.at[:, m, c, :], raw.at[c, :, pl.ds(m * Q, Q)]))
-    loads += [(first_hbm, first), (tc_hbm, tc), (ts_hbm, ts), (fwd_hbm, fwd), (tmpl_hbm, tmpl)]
-    loads = [pltpu.make_async_copy(s, d, load_sem.at[i]) for i, (s, d) in enumerate(loads)]
-    for load in loads[: 2 * RADIX + 1]:
-        load.start()
 
     barrier = pltpu.get_barrier_semaphore()
     for dx, pair in BANK_PEERS:
@@ -359,12 +359,11 @@
         axis=0,
     )
     for o in range(owners):
-        parts = []
-        for i in range(o * per, (o + 1) * per):
-            low = i // RADIX * 8
-            parts.append(power[i % RADIX][low : low + 8])
-        parts += [extra, jnp.zeros((8, Q), jnp.float32)]
-        send[o] = half(jnp.concatenate(parts, axis=0))
+        for i in range(per):
+            tile = o * per + i
+            low = tile // RADIX * 8
+            send[o, i] = half(power[tile % RADIX][low : low + 8])
+        send[o, per] = half(extra)
 
     def sum_copy(i, device, slot):
         return pltpu.make_async_remote_copy(
@@ -405,15 +404,15 @@
 
     region(1, blocks[1], blocks[0])
 
-    total = full(send[own])
+    total = [full(send[own, i]) for i in range(per + 1)]
     for copy in sums:
         copy.wait_recv()
-    for i in range(tm - 1):
-        total = total + full(recv[i])
-    weight = lax.rsqrt(total * (1.0 / total_blocks) + epsilon)
+    for k in range(tm - 1):
+        total = [x + full(recv[k, i]) for i, x in enumerate(total)]
+    weight = [lax.rsqrt(x * (1.0 / total_blocks) + epsilon) for x in total]
     mine = pl.ds(b * tiles + own * per, per)
     for i in range(per):
-        weights[b * tiles + own * per + i] = half(weight[8 * i : 8 * i + 8])
+        weights[b * tiles + own * per + i] = half(weight[i])
 
     for d in NEARER_HALF:
         pltpu.make_async_remote_copy(
@@ -460,7 +459,7 @@
             for p in range(2):
                 lanes = fill_slot(2 * r + p, Q)
                 z_ref[q, HALF:ROWS, lanes] = half(
-                    zraw[q, HALF:ROWS, lanes] * weight[8 * per + r : 8 * per + r + 1]
+                    zraw[q, HALF:ROWS, lanes] * weight[per][r : r + 1]
                 )
 
     for copy in outgoing:
@@ -505,8 +504,8 @@
             pltpu.VMEM((ROWS, R), f32),
             pltpu.VMEM((RADIX, HALF, HALF), bf),
             pltpu.VMEM((2, ROWS, 2 * R), f32),
-            pltpu.VMEM((tm // 2, 32, Q), bf),
-            pltpu.VMEM((tm - 1, 32, Q), bf),
+            pltpu.VMEM((tm // 2, 3, 8, Q), bf),
+            pltpu.VMEM((tm - 1, 3, 8, Q), bf),
             pltpu.VMEM((HALF // 8 * RADIX, 8, Q), bf),
             sem((2 * RADIX + 6,)),
             sem((bank - 1,)),

time: 33 us -> 32.8 us (level)
  no operation moved by 1% of the time
where the time goes in v6:
time: 32.8 us; the launch traced here: 32.7 us
  Pallas kernels  32.7 us (100%)
    pallas_call x1, Pallas kernels, spectra(): pl.pallas_call(functools.partial(spectrum_kernel, tm, bank, 2 * tm), in_s...  27.6 us
    pallas_call x1, Pallas kernels, inverse(): pl.pallas_call(functools.partial(inverse_kernel, n), in_specs=[pl.BlockSp...  5.09 us

profile of v6, /device:TPU:1, one launch (start us, length us, event | category | flops | bytes accessed | tf_op | source)
XLA Modules:
  0.0 32.7 jit_solution(126065806961607174)
XLA Ops:
  0.0 0.0 copy-start.1
  0.0 0.0 copy-start
  0.0 27.6 %spectra.1 = (bf16[2,272,1024]{2,1,0:T(8,128)(2,1)S(1)}, bf16[4,272,1024]{2,1,0:T(8,128)(2,1)S(1)}, bf16[272,512]{1,0:T(8,128)(2,1)S(1)}, bf16[272,512]{1,0:T(8,128)(2,1)S(1)}) custom-call(f32[32,4,2,128]{3,2,1,0:T(2,128)} %bitcast.10, s32[2]{0:T(128)} %lens_hbm.1, bf16[2,4,512,512]{3,2,1,0:T(8,128)(2,1)} %tmpl_hbm.1, ...), custom_call_target="tpu_custom_call" | custom-call | tf_op jit(solution)/shard_map/spectra/pallas_call | solution.py:486
  27.6 0.0 copy-done.1
  27.6 0.0 copy-done
  27.6 5.1 %inverse.1 = f32[512,4,4,128]{3,2,1,0:T(4,128)} custom-call(bf16[2,272,1024]{2,1,0:T(8,128)(2,1)S(1)} %get-tuple-element.9.z_ref, bf16[4,272,1024]{2,1,0:T(8,128)(2,1)S(1)} %get-tuple-element.10.g_ref, bf16[4,256,256]{2,1,0:T(8,128)(2,1)S(1)} %copy-done, bf16[272,512]{1,0:T(8,128)(2,1)S(1)} %get-tuple-element.11.tc_ref, ...), custom_call_target="tpu_custom_call" | custom-call | tf_op jit(solution)/shard_map/inverse/pallas_call | solution.py:130
Async XLA Ops:
  0.0 27.6 %copy-start.1 = (bf16[256,512]{1,0:T(8,128)(2,1)S(1)}, bf16[256,512]{1,0:T(8,128)(2,1)}, u32[]{:S(2)}) copy-start(bf16[256,512]{1,0:T(8,128)(2,1)} %constant.17.clone.last_ref) | copy-start | bytes 786436
  0.0 27.6 %copy-start = (bf16[4,256,256]{2,1,0:T(8,128)(2,1)S(1)}, bf16[4,256,256]{2,1,0:T(8,128)(2,1)}, u32[]{:S(2)}) copy-start(bf16[4,256,256]{2,1,0:T(8,128)(2,1)} %constant.16.clone.inv_ref) | copy-start | bytes 1572868

commit v7 on v6

--- a/solution.py
+++ b/solution.py
@@ -99,11 +99,14 @@
     copies = []
 
     def last_rows(j, q):
-        y[j, pl.ds(q * HALF, HALF)] = dot(last_ref[...], back[j % 2, q])
-        if q == 0 and j < n - 1:
-            return
-        at, size = (0, 2 * HALF) if j < n - 1 else (q * HALF, HALF)
+        final = j == n - 1
+        at, size = (q * HALF, HALF) if final else (0, 2 * HALF)
         for m in range(RADIX):
+            if m % 2 == 0:
+                lanes = pl.ds(m * Q, 2 * Q)
+                y[j, pl.ds(q * HALF, HALF), lanes] = dot(last_ref[...], back[j % 2, q, :, lanes])
+            if q == 0 and not final:
+                continue
             copy = pltpu.make_async_copy(
                 y.at[j, pl.ds(at, size), pl.ds(m * Q, Q)],
                 out_ref.at[pl.ds(at, size), m, j, :],

time: 32.8 us -> 34.1 us (1.040)
  Pallas kernels: 32.7 us -> 34 us
    pallas_call x1, Pallas kernels: 5.09 us -> 6.39 us  [inverse(): pl.pallas_call(functools.partial(inverse_kernel, n), in_specs=[pl.BlockSp...]
where the time goes in v7:
time: 34.1 us; the launch traced here: 34 us
  Pallas kernels  34 us (100%)
    pallas_call x1, Pallas kernels, spectra(): pl.pallas_call(functools.partial(spectrum_kernel, tm, bank, 2 * tm), in_s...  27.6 us
    pallas_call x1, Pallas kernels, inverse(): pl.pallas_call(functools.partial(inverse_kernel, n), in_specs=[pl.BlockSp...  6.39 us

profile of v7, /device:TPU:1, one launch (start us, length us, event | category | flops | bytes accessed | tf_op | source)
XLA Modules:
  0.0 34.0 jit_solution(8152717195847639184)
XLA Ops:
  0.0 0.0 copy-start.1
  0.0 0.0 copy-start
  0.0 27.6 %spectra.1 = (bf16[2,272,1024]{2,1,0:T(8,128)(2,1)S(1)}, bf16[4,272,1024]{2,1,0:T(8,128)(2,1)S(1)}, bf16[272,512]{1,0:T(8,128)(2,1)S(1)}, bf16[272,512]{1,0:T(8,128)(2,1)S(1)}) custom-call(f32[32,4,2,128]{3,2,1,0:T(2,128)} %bitcast.10, s32[2]{0:T(128)} %lens_hbm.1, bf16[2,4,512,512]{3,2,1,0:T(8,128)(2,1)} %tmpl_hbm.1, ...), custom_call_target="tpu_custom_call" | custom-call | tf_op jit(solution)/shard_map/spectra/pallas_call | solution.py:489
  27.6 0.0 copy-done.1
  27.6 0.0 copy-done
  27.6 6.4 %inverse.1 = f32[512,4,4,128]{3,2,1,0:T(4,128)} custom-call(bf16[2,272,1024]{2,1,0:T(8,128)(2,1)S(1)} %get-tuple-element.9.z_ref, bf16[4,272,1024]{2,1,0:T(8,128)(2,1)S(1)} %get-tuple-element.10.g_ref, bf16[4,256,256]{2,1,0:T(8,128)(2,1)S(1)} %copy-done, bf16[272,512]{1,0:T(8,128)(2,1)S(1)} %get-tuple-element.11.tc_ref, ...), custom_call_target="tpu_custom_call" | custom-call | tf_op jit(solution)/shard_map/inverse/pallas_call | solution.py:133
Async XLA Ops:
  0.0 27.6 %copy-start.1 = (bf16[256,512]{1,0:T(8,128)(2,1)S(1)}, bf16[256,512]{1,0:T(8,128)(2,1)}, u32[]{:S(2)}) copy-start(bf16[256,512]{1,0:T(8,128)(2,1)} %constant.17.clone.last_ref) | copy-start | bytes 786436
  0.0 27.6 %copy-start = (bf16[4,256,256]{2,1,0:T(8,128)(2,1)S(1)}, bf16[4,256,256]{2,1,0:T(8,128)(2,1)}, u32[]{:S(2)}) copy-start(bf16[4,256,256]{2,1,0:T(8,128)(2,1)} %constant.16.clone.inv_ref) | copy-start | bytes 1572868
